TPU v7x, 512 devices: a whole 4x8x8 slice. The times are simulated.
512 devices in a mesh: section: 4 (over x), ctx: 64 (over y, z), mp: 2 (over core).
Axes of the slice: x: 4, y: 8, z: 8, core: 2. Of those that a mesh axis runs over, the one named last changes fastest.
Arguments:
- head_input: bfloat16 [4, 16384, 2048], P('section', 'ctx', 'mp'), may hold values from -6 to 6
- state_proj: bfloat16 [4, 16384, 256], P('section', 'ctx'), may hold values from -6 to 6
- gate_input: bfloat16 [4, 16384, 2048], P('section', 'ctx', 'mp'), may hold values from -6 to 6
- step_raw: float32 [4, 32, 16384], P('section', 'mp', 'ctx'), may hold values from -2 to 2
- step_bias: float32 [4, 32], P('section', 'mp'), may hold values from -9.5 to -3
- decay_log: float32 [4, 32], P('section', 'mp'), may hold values from -7 to 1.5
- skip_gain: float32 [4, 32], P('section', 'mp'), may hold values from 0.5 to 1.5
- conv_head: float32 [4, 4, 2048], P('section', None, 'mp'), may hold values from -3 to 3
- conv_state: float32 [4, 4, 256], P('section'), may hold values from -3 to 3
- norm_gain: float32 [4, 2048], P('section', 'mp'), may hold values from 0.1 to 1.9
- next_weight: bfloat16 [4, 2048, 4096], P('section', 'ctx', 'mp'), may hold values from -0.125 to 0.125
Outputs:
- projected: bfloat16 [4, 16384, 4096], P('section', 'ctx', 'mp')
All inputs are finite; a program needn't handle non-finite values.
Results may differ from a plain program's by a relative error of at most 0.0087.
Values may be sent and summed in bfloat16 or wider, within the bound.
No kernel may reach another device: no remote copies, remote signals or barrier semaphores. Data moves between devices by JAX's collectives and lax.ppermute only.
A program may use at most 64 MiB of HBM per device.

v0:
```python
import jax
import jax.numpy as jnp
from jax import lax
from jax.sharding import Mesh
from jax.sharding import PartitionSpec as P

STATE = 128
BLOCK = 256
FEATURES = 2048
CTX = ("ctx_0", "ctx_1")


NORM_FLOOR = 0.25
HIGHEST = lax.Precision.HIGHEST


def from_behind(value, axis, steps):
    count = lax.axis_size(axis)
    first, last = (max(0, -steps), min(count, count - steps))
    return lax.ppermute(value, axis, [(source, source + steps) for source in range(first, last)])


def nothing_yet(x, identity):
    return jax.tree.map(
        lambda part, zero: jnp.zeros_like(part) + jnp.asarray(zero, part.dtype), x, identity
    )


def prefix_by_axis(x, axes, combine, identity):
    before = start = nothing_yet(x, identity)
    running = x
    for axis in reversed(axes):
        devices, mine = (lax.axis_size(axis), lax.axis_index(axis))
        pieces = jax.tree.map(
            lambda part, kind: lax.all_gather(part.astype(kind), axis),
            running,
            (jnp.bfloat16, jnp.bfloat16),
        )
        inside, running = (start, start)
        for k in range(devices):
            passed = k < mine
            running = combine(
                running, jax.tree.map(lambda part, own: part[k].astype(own.dtype), pieces, x)
            )
            inside = jax.tree.map(lambda new, old: jnp.where(passed, new, old), running, inside)
        before = combine(inside, before)
    return before


def gathered_total(x, axis):
    return lax.all_gather(x, axis).sum(0)


def sent_to_all(x, axis):
    copies = jnp.broadcast_to(x, (lax.axis_size(axis), *x.shape))
    return lax.all_to_all(copies, axis, split_axis=0, concat_axis=0, tiled=True)


def in_order(pieces, dim):
    pieces = jnp.moveaxis(pieces, 0, dim)
    lengths = pieces.shape
    return pieces.reshape(*lengths[:dim], lengths[dim] * lengths[dim + 1], *lengths[dim + 2 :])


def collect(x, axis, dim):
    pieces = sent_to_all(x, axis)
    return in_order(pieces, dim)


def shifted(value, axis, steps):
    count = lax.axis_size(axis)
    pairs = [(source, (source + steps) % count) for source in range(count)]
    return lax.ppermute(value, axis, pairs)


def causal_conv(sequence, previous, weights):
    length = sequence.shape[0]
    padded = jnp.concatenate([previous, sequence], axis=0).astype(jnp.float32)
    summed = jnp.zeros(sequence.shape, jnp.float32)
    for offset in range(weights.shape[0]):
        summed = summed + weights[offset] * padded[offset : offset + length]
    return summed


def chain_step(earlier, latter):
    return (earlier[0] + latter[0], jnp.exp(latter[0])[:, None, None] * earlier[1] + latter[1])


def shards(
    head_input,
    state_proj,
    gate_input,
    step_raw,
    step_bias,
    decay_log,
    skip_gain,
    conv_head,
    conv_state,
    norm_gain,
    next_weight,
):
    tap_count = conv_head.shape[1]
    token_count = head_input.shape[1]
    local_width = head_input.shape[2]
    head_count = step_raw.shape[1]
    head_width = local_width // head_count
    block_count = token_count // BLOCK
    tails = jnp.concatenate(
        [
            head_input[0, token_count - tap_count + 1 :],
            state_proj[0, token_count - tap_count + 1 :],
        ],
        axis=1,
    )
    previous = from_behind(tails, CTX, 1)
    conv_x = jax.nn.silu(
        causal_conv(head_input[0], previous[:, :local_width], conv_head[0])
    ).astype(jnp.bfloat16)
    conv_bc = causal_conv(state_proj[0], previous[:, local_width:], conv_state[0]).astype(
        jnp.bfloat16
    )
    blocks_x = conv_x.reshape(block_count, BLOCK, head_count, head_width)
    blocks_b = conv_bc[:, :STATE].reshape(block_count, BLOCK, STATE)
    blocks_c = conv_bc[:, STATE:].reshape(block_count, BLOCK, STATE)
    step_size = jax.nn.softplus(step_raw[0] + step_bias[0][:, None])
    log_decay = -jnp.exp(decay_log[0])[:, None] * step_size
    blocks_step = step_size.reshape(head_count, block_count, BLOCK)
    blocks_decay = log_decay.reshape(head_count, block_count, BLOCK)
    row_index = lax.broadcasted_iota(jnp.int32, (BLOCK, BLOCK), 0)
    col_index = lax.broadcasted_iota(jnp.int32, (BLOCK, BLOCK), 1)
    causal_mask = row_index >= col_index
    lower_tri = causal_mask.astype(jnp.float32)
    cumulative = jnp.einsum("hcs,ts->hct", blocks_decay, lower_tri, precision=HIGHEST)
    scores = jnp.einsum("ctn,csn->cts", blocks_c, blocks_b, preferred_element_type=jnp.float32)
    decay_diff = jnp.where(causal_mask, cumulative[..., :, None] - cumulative[..., None, :], 0.0)
    mix_weight = jnp.where(
        causal_mask, scores[None] * jnp.exp(decay_diff) * blocks_step[:, :, None, :], 0.0
    ).astype(jnp.bfloat16)
    intra_part = jnp.einsum(
        "hcts,cshp->cthp", mix_weight, blocks_x, preferred_element_type=jnp.float32
    )
    tail_weight = jnp.exp(cumulative[..., -1:] - cumulative) * blocks_step
    weighted_b = (blocks_b.astype(jnp.float32)[None] * tail_weight[..., None]).astype(jnp.bfloat16)
    updates = jnp.einsum(
        "cshp,hcsn->chpn", blocks_x, weighted_b, preferred_element_type=jnp.float32
    )
    totals = cumulative[..., -1]
    running = jnp.zeros((head_count, head_width, STATE), jnp.float32)
    before = jnp.zeros((head_count,), jnp.float32)
    entering = running
    offsets = before
    running = jnp.exp(totals[:, 0])[:, None, None] * running + updates[0]
    before = totals[:, 0]
    prior_log, prior_state = prefix_by_axis(
        (before, running), CTX, chain_step, (jnp.zeros_like(before), jnp.zeros_like(running))
    )
    full_states = jnp.stack([entering + jnp.exp(offsets)[:, None, None] * prior_state])
    inter_part = (
        jnp.einsum("ctn,chpn->cthp", blocks_c.astype(jnp.float32), full_states, precision=HIGHEST)
        * jnp.exp(cumulative).transpose(1, 2, 0)[..., None]
    )
    output = (
        intra_part + inter_part + skip_gain[0][None, None, :, None] * blocks_x.astype(jnp.float32)
    )
    gated = output.reshape(token_count, local_width) * jax.nn.silu(
        gate_input[0].astype(jnp.float32)
    )
    squares = gathered_total(jnp.sum(gated * gated, axis=1), "mp")
    mean_square = squares / FEATURES
    normed = (gated * lax.rsqrt(mean_square + NORM_FLOOR)[:, None] * norm_gain[0][None]).astype(
        jnp.bfloat16
    )
    gathered = collect(normed, "mp", 1)
    arrived = shifted(gathered, "section", 1)
    weight_rows = next_weight[0]
    full_weight = lax.all_gather(weight_rows, CTX, axis=0, tiled=True)
    result = jnp.dot(arrived, full_weight, preferred_element_type=jnp.float32)
    return result.astype(jnp.bfloat16)[None]


def solution(mesh):
    finer = Mesh(
        mesh.devices.reshape(mesh.shape["section"], 8, 8, mesh.shape["mp"]),
        ("section", "ctx_0", "ctx_1", "mp"),
    )
    in_specs = (
        P("section", CTX, "mp"),
        P("section", CTX, None),
        P("section", CTX, "mp"),
        P("section", "mp", CTX),
        P("section", "mp"),
        P("section", "mp"),
        P("section", "mp"),
        P("section", None, "mp"),
        P("section", None, None),
        P("section", "mp"),
        P("section", CTX, "mp"),
    )
    out_specs = P("section", CTX, "mp")
    return jax.shard_map(
        shards, mesh=finer, in_specs=in_specs, out_specs=out_specs, check_vma=False
    )
```

profile of v0, /device:TPU:1, one launch (start us, length us, event | category | flops | bytes accessed | tf_op | source)
XLA Modules:
  0.0 230.0 jit_solution(1536751369088576350)
XLA Ops:
  6.5 0.7 slice_bitcast_fusion.16
  7.3 0.7 slice_bitcast_fusion.17
  8.0 4.8 %collective-permute-start = (bf16[3,1280]{1,0:T(4,128)(2,1)S(1)}, bf16[3,1280]{1,0:T(4,128)(2,1)S(1)}, u32[]{:S(2)}, u32[]{:S(2)}) collective-permute-start(bf16[3,1280]{1,0:T(4,128)(2,1)S(1)} %pad_maximum_fusion), channel_id=1, source_target_pairs={{0,2},{2,4},{4,6},{6,8},{8,10},{10,12},{12,14},{14,16},{16,18},{18... | collective-permute-start | bytes 23048 | tf_op jit(solution)/shard_map/ppermute | solution.py:20
  12.8 0.7 negate_bitcast_fusion
  13.4 0.9 fusion.159
  14.3 0.8 compare_select_fusion
  15.3 0.3 multiply_reduce_fusion.1
  15.6 0.8 exponential_multiply_fusion
  16.4 0.8 fusion.160
  17.3 1.2 copy.20
  18.8 0.9 maximum_convert_fusion.1
  19.9 0.3 maximum_convert_fusion
  20.2 1.6 multiply_convert_fusion.2
  21.8 1.5 fusion.19
  23.5 1.3 dynamic-slice
  25.5 0.2 dynamic-update-slice
  25.7 17.4 %all-reduce = bf16[128]{0:T(256)(128)(2,1)S(1)} all-reduce(bf16[128]{0:T(256)(128)(2,1)S(1)} %dynamic-update-slice), channel_id=2, replica_groups=mesh['section'=4,'ctx_0'=8,'ctx_1'=8,'mp'=2] {'ctx_1'}, use_global_device_ids=true, to_apply=%add | all-reduce | flops 128 | bytes 512
  43.3 24.0 %all-gather.12.cloned.1.call-done = bf16[128,64,128]{2,1,0:T(8,128)(2,1)} async-done(((bf16[16,64,128]{2,1,0:T(8,128)(2,1)}), bf16[128,64,128]{2,1,0:T(8,128)(2,1)}) %all-gather.12.cloned.1.call-update) | async-done | bytes 2097168 | tf_op jit(solution)/shard_map/all_gather | solution.py:35
  67.4 2.8 %fusion.76 = bf16[1,16,64,128]{3,2,1,0:T(8,128)(2,1)} fusion(f32[16]{0:T(128)S(1)} %get-tuple-element.33, f32[16]{0:T(128)S(1)} %get-tuple-element.32, f32[16]{0:T(128)S(1)} %get-tuple-element.31, f32[16]{0:T(128)S(1)} %get-tuple-element.30, f32[16]{0:T(128)S(1)} %get-tuple-element.29, f32[16]{0:T(128)S(1)} %get-tuple-element.27, ...), kind=kLoop, calls=%fused_computation.93 | loop fusion | flops 3145728 | bytes 2359808 | tf_op jit(solution)/shard_map/convert_element_type | solution.py:35
  70.2 0.7 all-gather.14.cloned.1.call-update
  70.9 0.2 copy.22
  71.2 12.6 %all-gather.4 = bf16[8,1,16]{2,1,0:T(2,128)(2,1)S(1)} all-gather(bf16[1,1,16]{2,1,0:T(2,128)(2,1)S(1)} %convert_bitcast_fusion), channel_id=1, replica_groups=mesh['section'=4,'ctx_0'=8,'ctx_1'=8,'mp'=2] {'ctx_0'}, dimensions={0}, use_global_device_ids=true | all-gather | bytes 288 | tf_op jit(solution)/shard_map/all_gather | solution.py:35
  84.0 27.9 %all-gather.10.cloned.1.call-done = bf16[8,16,64,128]{3,2,1,0:T(8,128)(2,1)} async-done(((bf16[1,16,64,128]{3,2,1,0:T(8,128)(2,1)}), bf16[8,16,64,128]{3,2,1,0:T(8,128)(2,1)}) %all-gather.10.cloned.1.call-update) | async-done | bytes 2097168 | tf_op jit(solution)/shard_map/all_gather | solution.py:35
  111.9 3.6 %fusion.16 = f32[1,256,16,64]{1,3,2,0:T(8,128)S(1)} fusion(f32[256,16]{0,1:T(8,128)S(1)} %get-tuple-element.8, bf16[8,16,64,128]{3,2,1,0:T(8,128)(2,1)} %all-gather.10.cloned.1.call-done, f32[16]{0:T(128)S(1)} %get-tuple-element.33, f32[16]{0:T(128)S(1)} %get-tuple-element.32, f32[16]{0:T(128)S(1)} %get-tuple-element.31, f32[16]{0:T(128)S(1)} %get-tuple-element.30, ...), kind=kOutput, calls=%fused_computation.15 | convolution fusion | flops 411303936 | bytes 5333520 | tf_op jit(solution)/shard_map/ctn,chpn->cthp/dot_general | solution.py:159
  115.5 1.6 multiply_reduce_fusion
  117.2 6.3 %all-gather.5 = f32[2,1,256]{2,1,0:T(1,128)S(1)} all-gather(f32[1,1,256]{2,1,0:T(1,128)S(1)} %bitcast.274), channel_id=4, replica_groups=mesh['section'=4,'ctx_0'=8,'ctx_1'=8,'mp'=2] {'mp'}, dimensions={0}, use_global_device_ids=true | all-gather | bytes 3072 | tf_op jit(solution)/shard_map/all_gather | solution.py:51
  123.6 0.4 fusion.31
  124.0 4.5 %all_to_all.5 = bf16[2,256,1024]{1,2,0:T(8,128)(2,1)S(1)} all-to-all(bf16[2,256,1024]{1,2,0:T(8,128)(2,1)S(1)} %broadcast_in_dim.18), channel_id=1, replica_groups=mesh['section'=4,'ctx_0'=8,'ctx_1'=8,'mp'=2] {'mp'}, dimensions={0} | all-to-all | bytes 2097152 | tf_op jit(solution)/shard_map/all_to_all | solution.py:56
  128.6 3.1 %collective-permute-start.1 = (bf16[256,2048]{0,1:T(8,128)(2,1)S(1)}, bf16[256,2048]{0,1:T(8,128)(2,1)S(1)}, u32[]{:S(2)}, u32[]{:S(2)}) collective-permute-start(bf16[256,2048]{0,1:T(8,128)(2,1)S(1)} %bitcast.256), channel_id=1, source_target_pairs={{0,128},{128,256},{256,384},{384,0},{1,129},{129,257},{257,385},{3... | collective-permute-start | bytes 3145736 | tf_op jit(solution)/shard_map/ppermute | solution.py:73
  131.6 24.3 %collective-permute-done.1 = bf16[256,2048]{0,1:T(8,128)(2,1)S(1)} collective-permute-done((bf16[256,2048]{0,1:T(8,128)(2,1)S(1)}, bf16[256,2048]{0,1:T(8,128)(2,1)S(1)}, u32[]{:S(2)}, u32[]{:S(2)}) %collective-permute-start.1) | collective-permute-done | bytes 1048608 | tf_op jit(solution)/shard_map/ppermute | solution.py:73
  156.0 60.8 %all-gather.14.cloned.1.call-done = bf16[1,2048,2048]{2,1,0:T(8,128)(2,1)} async-done(((bf16[1,32,2048]{2,1,0:T(8,128)(2,1)}), bf16[1,2048,2048]{2,1,0:T(8,128)(2,1)}) %all-gather.14.cloned.1.call-update) | async-done | bytes 8388624 | tf_op jit(solution)/shard_map/all_gather | solution.py:176
  216.8 6.7 %fusion.5 = bf16[1,256,2048]{2,1,0:T(8,128)(2,1)} fusion(bf16[256,2048]{0,1:T(8,128)(2,1)S(1)} %collective-permute-done.1, bf16[1,2048,2048]{2,1,0:T(8,128)(2,1)} %all-gather.14.cloned.1.call-done), kind=kOutput, calls=%fused_computation.4 | convolution fusion | flops 2148007936 | bytes 10485760 | tf_op jit(solution)/shard_map/dot_general | solution.py:177
  (31 shorter events, 1.5 us)
Async XLA Ops:
  6.5 60.8 %all-gather.12.cloned.1.call-start = ((), (), s32[]{:S(2)}) async-start(), calls=%async_computation.2 | async-start | bytes 2359296 | tf_op jit(solution)/shard_map/all_gather | solution.py:35
  8.0 10.6 %collective-permute-start = (bf16[3,1280]{1,0:T(4,128)(2,1)S(1)}, bf16[3,1280]{1,0:T(4,128)(2,1)S(1)}, u32[]{:S(2)}, u32[]{:S(2)}) collective-permute-start(bf16[3,1280]{1,0:T(4,128)(2,1)S(1)} %pad_maximum_fusion), channel_id=1, source_target_pairs={{0,2},{2,4},{4,6},{6,8},{8,10},{10,12},{12,14},{14,16},{16,18},{18... | collective-permute-start | bytes 23048 | tf_op jit(solution)/shard_map/ppermute | solution.py:20
  21.8 49.1 %copy-start = (bf16[1,256,1024]{2,1,0:T(8,128)(2,1)S(1)}, bf16[1,256,1024]{2,1,0:T(8,128)(2,1)}, u32[]{:S(2)}) copy-start(bf16[1,256,1024]{2,1,0:T(8,128)(2,1)} %param.13) | copy-start | bytes 1572868
  23.4 88.5 %all-gather.10.cloned.1.call-start = ((), (), s32[]{:S(2)}) async-start(), calls=%async_computation.1 | async-start | bytes 2359296 | tf_op jit(solution)/shard_map/all_gather | solution.py:35
  70.2 146.6 %all-gather.14.cloned.1.call-start = ((), (), s32[]{:S(2)}) async-start(), calls=%async_computation.3 | async-start | bytes 8519680 | tf_op jit(solution)/shard_map/all_gather | solution.py:176
  111.9 3.6 %copy-start.2 = (f32[1,16]{1,0:T(1,128)S(1)}, f32[1,16]{1,0:T(1,128)}, u32[]{:S(2)}) copy-start(f32[1,16]{1,0:T(1,128)} %param.17) | copy-start | bytes 196
  115.5 8.0 %copy-start.1 = (f32[1,1024]{1,0:T(1,128)S(1)}, f32[1,1024]{1,0:T(1,128)}, u32[]{:S(2)}) copy-start(f32[1,1024]{1,0:T(1,128)} %param.20) | copy-start | bytes 12292
  128.6 27.4 %collective-permute-start.1 = (bf16[256,2048]{0,1:T(8,128)(2,1)S(1)}, bf16[256,2048]{0,1:T(8,128)(2,1)S(1)}, u32[]{:S(2)}, u32[]{:S(2)}) collective-permute-start(bf16[256,2048]{0,1:T(8,128)(2,1)S(1)} %bitcast.256), channel_id=1, source_target_pairs={{0,128},{128,256},{256,384},{384,0},{1,129},{129,257},{257,385},{3... | collective-permute-start | bytes 3145736 | tf_op jit(solution)/shard_map/ppermute | solution.py:73
Sparse Core Ops, SparseCore 0:
  23.5 43.8 all-gather.11
  70.3 41.5 all-gather.9
  114.9 101.8 all-gather.13
where the time goes:
time: 231 us; the launch traced here: 230 us
  waiting for transfers between devices  138 us (60%)
  blocking collectives  40.8 us (18%)
  between operations  13.9 us (6%)
  matrix products  13.8 us (6%)
  other arithmetic  9.13 us (4%)
  starting transfers between devices  7.98 us (3%)
  local copies, waits for them, and re-layouts  6.58 us (3%)
    all_gather x1, waiting for transfers between devices, shards(): full_weight = lax.all_gather(weight_rows, CTX, axis=0, tiled=True)  60.8 us
    all_gather x2, waiting for transfers between devices, prefix_by_axis(): lax.all_gather(part.astype(kind), axis)  51.9 us
    ppermute x1, waiting for transfers between devices, shifted(): return lax.ppermute(value, axis, pairs)  24.3 us
    unnamed x1, blocking collectives  17.4 us
    all_gather x1, blocking collectives, prefix_by_axis(): lax.all_gather(part.astype(kind), axis)  12.6 us
    dot_general x1, matrix products, shards(): result = jnp.dot(arrived, full_weight, preferred_element_type=jnp.float32)  6.7 us
    all_gather x1, blocking collectives, gathered_total(): return lax.all_gather(x, axis).sum(0)  6.34 us
    ppermute x1, starting transfers between devices, from_behind(): lax.ppermute(value, axis, [(source, source + steps) for source in range(f...  4.81 us
  transfers between devices with their start and end apart: 5, of which 4 were waited for; matrix products, arithmetic and copies ran while one was open for 6% of the time, Pallas kernels for 0%

commit v1 on v0

--- a/solution.py
+++ b/solution.py
@@ -1,6 +1,8 @@
 import jax
 import jax.numpy as jnp
 from jax import lax
+from jax.experimental import pallas as pl
+from jax.experimental.pallas import tpu as pltpu
 from jax.sharding import Mesh
 from jax.sharding import PartitionSpec as P
 
@@ -20,51 +22,53 @@
     return lax.ppermute(value, axis, [(source, source + steps) for source in range(first, last)])
 
 
-def nothing_yet(x, identity):
-    return jax.tree.map(
-        lambda part, zero: jnp.zeros_like(part) + jnp.asarray(zero, part.dtype), x, identity
-    )
+def split_in_two(x):
+    high = lax.reduce_precision(x, 8, 7)
+    return high.astype(jnp.bfloat16), (x - high).astype(jnp.bfloat16)
 
 
-def prefix_by_axis(x, axes, combine, identity):
-    before = start = nothing_yet(x, identity)
-    running = x
-    for axis in reversed(axes):
-        devices, mine = (lax.axis_size(axis), lax.axis_index(axis))
-        pieces = jax.tree.map(
-            lambda part, kind: lax.all_gather(part.astype(kind), axis),
-            running,
-            (jnp.bfloat16, jnp.bfloat16),
+def scan_kernel(pieces_ref, prior_ref):
+    count, _, width = pieces_ref.shape
+    rows = prior_ref.shape[1]
+    carried = jnp.zeros((rows, width), jnp.float32)
+    for k in range(count):
+        prior_ref[k] = carried.astype(jnp.bfloat16)
+        factor = pieces_ref[k, rows : rows + 2, :].astype(jnp.float32)
+        carried = (factor[0:1] + factor[1:2]) * carried + pieces_ref[k, 0:rows, :].astype(
+            jnp.float32
         )
-        inside, running = (start, start)
-        for k in range(devices):
-            passed = k < mine
-            running = combine(
-                running, jax.tree.map(lambda part, own: part[k].astype(own.dtype), pieces, x)
-            )
-            inside = jax.tree.map(lambda new, old: jnp.where(passed, new, old), running, inside)
-        before = combine(inside, before)
-    return before
+
+
+def states_before(state, total_log, axes):
+    count = lax.axis_size(axes)
+    head_count, head_width, width = state.shape
+    rows = head_count * head_width // count
+    slices = state.astype(jnp.bfloat16).reshape(count, rows, width)
+    high, low = split_in_two(jnp.exp(total_log))
+    factors = jnp.stack([high, low], axis=1)
+    factors = jnp.repeat(factors, count // head_count, axis=0)
+    factors = jnp.broadcast_to(factors[:, :, None], (count, 2, width))
+    sent = jnp.concatenate([slices, factors], axis=1)
+    pieces = lax.all_to_all(sent, axes, 0, 0, tiled=True)
+    prior = pl.pallas_call(
+        scan_kernel,
+        out_shape=jax.ShapeDtypeStruct((count, rows, width), jnp.bfloat16),
+        in_specs=[pl.BlockSpec(memory_space=pltpu.VMEM)],
+        out_specs=pl.BlockSpec(memory_space=pltpu.VMEM),
+        cost_estimate=pl.CostEstimate(
+            flops=3 * count * rows * width, bytes_accessed=4 * count * rows * width, transcendentals=0
+        ),
+    )(pieces)
+    back = lax.all_to_all(prior, axes, 0, 0, tiled=True)
+    return back.reshape(head_count, head_width, width)
+
+
+def other_half(x, axis):
+    return lax.ppermute(x, axis, [(0, 1), (1, 0)])
 
 
 def gathered_total(x, axis):
     return lax.all_gather(x, axis).sum(0)
-
-
-def sent_to_all(x, axis):
-    copies = jnp.broadcast_to(x, (lax.axis_size(axis), *x.shape))
-    return lax.all_to_all(copies, axis, split_axis=0, concat_axis=0, tiled=True)
-
-
-def in_order(pieces, dim):
-    pieces = jnp.moveaxis(pieces, 0, dim)
-    lengths = pieces.shape
-    return pieces.reshape(*lengths[:dim], lengths[dim] * lengths[dim + 1], *lengths[dim + 2 :])
-
-
-def collect(x, axis, dim):
-    pieces = sent_to_all(x, axis)
-    return in_order(pieces, dim)
 
 
 def shifted(value, axis, steps):
@@ -82,10 +86,6 @@
     return summed
 
 
-def chain_step(earlier, latter):
-    return (earlier[0] + latter[0], jnp.exp(latter[0])[:, None, None] * earlier[1] + latter[1])
-
-
 def shards(
     head_input,
     state_proj,
@@ -99,6 +99,7 @@
     norm_gain,
     next_weight,
 ):
+    full_weight = lax.all_gather(next_weight[0], CTX, axis=0, tiled=True)
     tap_count = conv_head.shape[1]
     token_count = head_input.shape[1]
     local_width = head_input.shape[2]
@@ -144,19 +145,9 @@
     updates = jnp.einsum(
         "cshp,hcsn->chpn", blocks_x, weighted_b, preferred_element_type=jnp.float32
     )
-    totals = cumulative[..., -1]
-    running = jnp.zeros((head_count, head_width, STATE), jnp.float32)
-    before = jnp.zeros((head_count,), jnp.float32)
-    entering = running
-    offsets = before
-    running = jnp.exp(totals[:, 0])[:, None, None] * running + updates[0]
-    before = totals[:, 0]
-    prior_log, prior_state = prefix_by_axis(
-        (before, running), CTX, chain_step, (jnp.zeros_like(before), jnp.zeros_like(running))
-    )
-    full_states = jnp.stack([entering + jnp.exp(offsets)[:, None, None] * prior_state])
+    prior_state = states_before(updates[0], cumulative[:, 0, -1], CTX)
     inter_part = (
-        jnp.einsum("ctn,chpn->cthp", blocks_c.astype(jnp.float32), full_states, precision=HIGHEST)
+        jnp.einsum("ctn,hpn->cthp", blocks_c, prior_state, preferred_element_type=jnp.float32)
         * jnp.exp(cumulative).transpose(1, 2, 0)[..., None]
     )
     output = (
@@ -170,11 +161,13 @@
     normed = (gated * lax.rsqrt(mean_square + NORM_FLOOR)[:, None] * norm_gain[0][None]).astype(
         jnp.bfloat16
     )
-    gathered = collect(normed, "mp", 1)
-    arrived = shifted(gathered, "section", 1)
-    weight_rows = next_weight[0]
-    full_weight = lax.all_gather(weight_rows, CTX, axis=0, tiled=True)
-    result = jnp.dot(arrived, full_weight, preferred_element_type=jnp.float32)
+    arrived = shifted(normed, "section", 1)
+    other = other_half(arrived, "mp")
+    low = lax.axis_index("mp") == 0
+    features = jnp.concatenate(
+        [jnp.where(low, arrived, other), jnp.where(low, other, arrived)], axis=1
+    )
+    result = jnp.dot(features, full_weight, preferred_element_type=jnp.float32)
     return result.astype(jnp.bfloat16)[None]
 
 

time: 231 us -> 134 us (0.58)
  waiting for transfers between devices: 138 us -> 42.3 us
  starting transfers between devices: 7.98 us -> 19.1 us
  blocking collectives: 40.8 us -> 35.4 us
  matrix products: 13.8 us -> 9.84 us
  other arithmetic: 9.13 us -> 5.86 us
    all_gather x3 -> x1, waiting for transfers between devices: 113 us -> 14.7 us  [shards(): full_weight = lax.all_gather(next_weight[0], CTX, axis=0, tiled=True)]
    all_to_all x1, blocking collectives: 4.54 us -> 30.6 us  [states_before(): pieces = lax.all_to_all(sent, axes, 0, 0, tiled=True)]
    unnamed x1 -> x0, blocking collectives: 17.4 us -> none
    all_gather x1 -> x0, blocking collectives: 12.6 us -> none  [prefix_by_axis(): lax.all_gather(part.astype(kind), axis)]
    all_to_all x0 -> x1, waiting for transfers between devices: none -> 12.1 us  [states_before(): back = lax.all_to_all(prior, axes, 0, 0, tiled=True)]
    ppermute x1, waiting for transfers between devices: 24.3 us -> 13.2 us  [shifted(): return lax.ppermute(value, axis, pairs)]
    all_to_all x0 -> x1, starting transfers between devices: none -> 8.14 us  [states_before(): back = lax.all_to_all(prior, axes, 0, 0, tiled=True)]
    dot_general x2, matrix products: 10.3 us -> 7 us  [the longest x1 6.7 us: shards(): result = jnp.dot(features, full_weight, preferred_element_type=jnp.float32)]
  transfers between devices with their start and end apart: 5 -> 5, of which waited for: 4 -> 4; matrix products, arithmetic and copies ran while one was open for 6% -> 11% of each run, Pallas kernels for 0% -> 1%
where the time goes in v1:
time: 134 us; the launch traced here: 133 us
  waiting for transfers between devices  42.3 us (32%)
  blocking collectives  35.4 us (26%)
  starting transfers between devices  19.1 us (14%)
  between operations  13.6 us (10%)
  matrix products  9.84 us (7%)
  other arithmetic  5.86 us (4%)
  local copies, waits for them, and re-layouts  5.32 us (4%)
  Pallas kernels  1.84 us (1%)
    all_to_all x1, blocking collectives, states_before(): pieces = lax.all_to_all(sent, axes, 0, 0, tiled=True)  30.6 us
    all_gather x1, waiting for transfers between devices, shards(): full_weight = lax.all_gather(next_weight[0], CTX, axis=0, tiled=True)  14.7 us
    ppermute x1, waiting for transfers between devices, shifted(): return lax.ppermute(value, axis, pairs)  13.2 us
    all_to_all x1, waiting for transfers between devices, states_before(): back = lax.all_to_all(prior, axes, 0, 0, tiled=True)  12.1 us
    all_to_all x1, starting transfers between devices, states_before(): back = lax.all_to_all(prior, axes, 0, 0, tiled=True)  8.14 us
    dot_general x1, matrix products, shards(): result = jnp.dot(features, full_weight, preferred_element_type=jnp.float32)  6.7 us
    ppermute x1, starting transfers between devices, from_behind(): lax.ppermute(value, axis, [(source, source + steps) for source in range(f...  4.81 us
    all_gather x1, blocking collectives, gathered_total(): return lax.all_gather(x, axis).sum(0)  4.81 us
  transfers between devices with their start and end apart: 5, of which 4 were waited for; matrix products, arithmetic and copies ran while one was open for 11% of the time, Pallas kernels for 1%

profile of v1, /device:TPU:1, one launch (start us, length us, event | category | flops | bytes accessed | tf_op | source)
XLA Modules:
  0.0 133.2 jit_solution(2932571899825449069)
XLA Ops:
  6.5 0.7 all-gather.5.cloned.1.call-update
  7.3 0.7 slice_bitcast_fusion.1
  8.0 0.7 slice_bitcast_fusion
  8.7 4.8 %collective-permute-start = (bf16[3,1280]{1,0:T(4,128)(2,1)S(1)}, bf16[3,1280]{1,0:T(4,128)(2,1)S(1)}, u32[]{:S(2)}, u32[]{:S(2)}) collective-permute-start(bf16[3,1280]{1,0:T(4,128)(2,1)S(1)} %pad_maximum_fusion.1), channel_id=1, source_target_pairs={{0,2},{2,4},{4,6},{6,8},{8,10},{10,12},{12,14},{14,16},{16,18},{18... | collective-permute-start | bytes 23048 | tf_op jit(solution)/shard_map/ppermute | solution.py:22
  13.5 0.7 negate_bitcast_fusion
  14.2 0.8 compare_select_fusion
  15.0 0.2 fusion.38
  15.2 0.3 slice_reduce_fusion
  15.5 0.8 fusion.50
  16.3 0.9 fusion.49
  17.2 0.8 exponential_bitcast_fusion
  18.0 1.2 copy.22
  19.4 0.2 copy.23
  19.6 0.9 maximum_convert_fusion.1
  20.5 0.3 maximum_convert_fusion
  21.1 1.6 %multiply_convert_fusion.2 = bf16[256,1024]{0,1:T(8,128)(2,1)S(1)} fusion(f32[259,1024]{0,1:T(8,128)S(1)} %maximum_convert_fusion, f32[1024]{0:T(1024)S(1)} %bitcast.104, f32[1024]{0:T(1024)S(1)} %bitcast.105, f32[1024]{0:T(1024)S(1)} %bitcast.103, f32[1024]{0:T(1024)S(1)} %bitcast.102), kind=kLoop, calls=%fused_computation.41 | loop fusion | flops 3145728 | bytes 4734976 | tf_op jit(solution)/shard_map/convert_element_type | solution.py:119
  22.7 0.8 convolution_convert_fusion
  23.7 30.6 %all_to_all.10.pieces_ref = bf16[64,18,128]{2,1,0:T(8,128)(2,1)} all-to-all(bf16[64,18,128]{2,1,0:T(8,128)(2,1)S(1)} %pad_maximum_fusion), channel_id=1, replica_groups=mesh['section'=4,'ctx_0'=8,'ctx_1'=8,'mp'=2] {'ctx_0','ctx_1'}, dimensions={0} | all-to-all | bytes 589824 | tf_op jit(solution)/shard_map/all_to_all | solution.py:52
  54.2 1.8 %shard_map.109 = bf16[64,16,128]{2,1,0:T(8,128)(2,1)} custom-call(bf16[64,18,128]{2,1,0:T(8,128)(2,1)} %all_to_all.10.pieces_ref), custom_call_target="tpu_custom_call" | custom-call | flops 393216 | bytes 524288 | tf_op jit(solution)/shard_map/pallas_call | solution.py:53
  56.1 8.1 %all-to-all-start.1 = ((bf16[64,16,128]{2,1,0:T(8,128)(2,1)}), bf16[64,16,128]{2,1,0:T(8,128)(2,1)S(1)}, u32[]{:S(2)}, u32[]{:S(2)}) async-start(bf16[64,16,128]{2,1,0:T(8,128)(2,1)} %shard_map.109), calls=%async_computation.1 | async-start | bytes 524288 | tf_op jit(solution)/shard_map/all_to_all | solution.py:62
  64.2 0.2 copy.25
  64.6 12.1 %all-to-all-done.1 = bf16[64,16,128]{2,1,0:T(8,128)(2,1)S(1)} async-done(((bf16[64,16,128]{2,1,0:T(8,128)(2,1)}), bf16[64,16,128]{2,1,0:T(8,128)(2,1)S(1)}, u32[]{:S(2)}, u32[]{:S(2)}) %all-to-all-start.1) | async-done | bytes 262176 | tf_op jit(solution)/shard_map/all_to_all | solution.py:62
  76.8 0.3 fusion.16
  77.1 1.7 %multiply_reduce_fusion = (f32[256]{0:T(256)S(1)}, f32[1,256,16,64]{1,3,2,0:T(8,128)S(1)}) fusion(bf16[1,256,16,64]{1,3,2,0:T(8,128)(2,1)S(1)} %bitcast.96, f32[16]{0:T(128)S(1)} %bitcast.114, f32[1,256,16,64]{1,3,2,0:T(8,128)S(1)} %fusion.16, bf16[256,16,64]{0,2,1:T(8,128)(2,1)S(1)} %bitcast.97, f32[16,256]{1,0:T(8,128)S(1)} %compare_select_fusion, ...), kind=kOutput, calls=%fused_computation.38 | convolution fusion | flops 143654656 | bytes 4031552 | tf_op jit(solution)/shard_map/hcts,cshp->cthp/dot_general | solution.py:140
  78.7 4.8 %all-gather.2 = f32[2,1,256]{2,1,0:T(1,128)S(1)} all-gather(f32[1,1,256]{2,1,0:T(1,128)S(1)} %bitcast.113), channel_id=2, replica_groups=mesh['section'=4,'ctx_0'=8,'ctx_1'=8,'mp'=2] {'mp'}, dimensions={0}, use_global_device_ids=true | all-gather | bytes 3072 | tf_op jit(solution)/shard_map/all_gather | solution.py:71
  83.6 0.4 fusion.33
  84.0 3.1 %collective-permute-start.1 = (bf16[256,1024]{0,1:T(8,128)(2,1)S(1)}, bf16[256,1024]{0,1:T(8,128)(2,1)S(1)}, u32[]{:S(2)}, u32[]{:S(2)}) collective-permute-start(bf16[256,1024]{0,1:T(8,128)(2,1)S(1)} %fusion.33), channel_id=1, source_target_pairs={{0,128},{128,256},{256,384},{384,0},{1,129},{129,257},{257,385},{3... | collective-permute-start | bytes 1572872 | tf_op jit(solution)/shard_map/ppermute | solution.py:77
  87.1 13.2 %collective-permute-done.1 = bf16[256,1024]{0,1:T(8,128)(2,1)S(1)} collective-permute-done((bf16[256,1024]{0,1:T(8,128)(2,1)S(1)}, bf16[256,1024]{0,1:T(8,128)(2,1)S(1)}, u32[]{:S(2)}, u32[]{:S(2)}) %collective-permute-start.1) | collective-permute-done | bytes 524320 | tf_op jit(solution)/shard_map/ppermute | solution.py:77
  100.3 3.0 %collective-permute-start.2 = (bf16[256,1024]{0,1:T(8,128)(2,1)S(1)}, bf16[256,1024]{0,1:T(8,128)(2,1)S(1)}, u32[]{:S(2)}, u32[]{:S(2)}) collective-permute-start(bf16[256,1024]{0,1:T(8,128)(2,1)S(1)} %collective-permute-done.1), channel_id=1, source_target_pairs={{0,1},{1,0},{2,3},{3,2},{4,5},{5,4},{6,7},{7,6},{8,9},{9,8},{10,11... | collective-permute-start | bytes 1572872 | tf_op jit(solution)/shard_map/ppermute | solution.py:67
  103.3 1.5 %collective-permute-done.2 = bf16[256,1024]{0,1:T(8,128)(2,1)S(1)} collective-permute-done((bf16[256,1024]{0,1:T(8,128)(2,1)S(1)}, bf16[256,1024]{0,1:T(8,128)(2,1)S(1)}, u32[]{:S(2)}, u32[]{:S(2)}) %collective-permute-start.2) | collective-permute-done | bytes 524320 | tf_op jit(solution)/shard_map/ppermute | solution.py:67
  104.9 14.7 %all-gather.5.cloned.1.call-done = bf16[1,2048,2048]{2,1,0:T(8,128)(2,1)} async-done(((bf16[1,32,2048]{2,1,0:T(8,128)(2,1)}), bf16[1,2048,2048]{2,1,0:T(8,128)(2,1)}) %all-gather.5.cloned.1.call-update) | async-done | bytes 8388624 | tf_op jit(solution)/shard_map/all_gather | solution.py:102
  119.6 6.7 %fusion.5 = bf16[1,256,2048]{2,1,0:T(8,128)(2,1)} fusion(bf16[1,2048,2048]{2,1,0:T(8,128)(2,1)} %all-gather.5.cloned.1.call-done, bf16[256,1024]{0,1:T(8,128)(2,1)S(1)} %get-tuple-element.8, bf16[256,1024]{0,1:T(8,128)(2,1)S(1)} %get-tuple-element.7), kind=kOutput, calls=%fused_computation.4 | convolution fusion | flops 2150105088 | bytes 10485760 | tf_op jit(solution)/shard_map/dot_general | solution.py:170
  (24 shorter events, 0.8 us)
Async XLA Ops:
  6.5 113.1 %all-gather.5.cloned.1.call-start = ((), (), s32[]{:S(2)}) async-start(), calls=%async_computation.2 | async-start | bytes 8519680 | tf_op jit(solution)/shard_map/all_gather | solution.py:102
  8.7 10.7 %collective-permute-start = (bf16[3,1280]{1,0:T(4,128)(2,1)S(1)}, bf16[3,1280]{1,0:T(4,128)(2,1)S(1)}, u32[]{:S(2)}, u32[]{:S(2)}) collective-permute-start(bf16[3,1280]{1,0:T(4,128)(2,1)S(1)} %pad_maximum_fusion.1), channel_id=1, source_target_pairs={{0,2},{2,4},{4,6},{6,8},{8,10},{10,12},{12,14},{14,16},{16,18},{18... | collective-permute-start | bytes 23048 | tf_op jit(solution)/shard_map/ppermute | solution.py:22
  21.0 43.2 %copy-start = (bf16[1,256,1024]{2,1,0:T(8,128)(2,1)S(1)}, bf16[1,256,1024]{2,1,0:T(8,128)(2,1)}, u32[]{:S(2)}) copy-start(bf16[1,256,1024]{2,1,0:T(8,128)(2,1)} %param.13) | copy-start | bytes 1572868
  22.6 54.4 %copy-start.2 = (f32[1,16]{1,0:T(1,128)S(1)}, f32[1,16]{1,0:T(1,128)}, u32[]{:S(2)}) copy-start(f32[1,16]{1,0:T(1,128)} %param.17) | copy-start | bytes 196
  56.1 20.7 %all-to-all-start.1 = ((bf16[64,16,128]{2,1,0:T(8,128)(2,1)}), bf16[64,16,128]{2,1,0:T(8,128)(2,1)S(1)}, u32[]{:S(2)}, u32[]{:S(2)}) async-start(bf16[64,16,128]{2,1,0:T(8,128)(2,1)} %shard_map.109), calls=%async_computation.1 | async-start | bytes 524288 | tf_op jit(solution)/shard_map/all_to_all | solution.py:62
  77.1 6.5 %copy-start.1 = (f32[1,1024]{1,0:T(1,128)S(1)}, f32[1,1024]{1,0:T(1,128)}, u32[]{:S(2)}) copy-start(f32[1,1024]{1,0:T(1,128)} %param.20) | copy-start | bytes 12292
  84.0 16.3 %collective-permute-start.1 = (bf16[256,1024]{0,1:T(8,128)(2,1)S(1)}, bf16[256,1024]{0,1:T(8,128)(2,1)S(1)}, u32[]{:S(2)}, u32[]{:S(2)}) collective-permute-start(bf16[256,1024]{0,1:T(8,128)(2,1)S(1)} %fusion.33), channel_id=1, source_target_pairs={{0,128},{128,256},{256,384},{384,0},{1,129},{129,257},{257,385},{3... | collective-permute-start | bytes 1572872 | tf_op jit(solution)/shard_map/ppermute | solution.py:77
  100.3 4.5 %collective-permute-start.2 = (bf16[256,1024]{0,1:T(8,128)(2,1)S(1)}, bf16[256,1024]{0,1:T(8,128)(2,1)S(1)}, u32[]{:S(2)}, u32[]{:S(2)}) collective-permute-start(bf16[256,1024]{0,1:T(8,128)(2,1)S(1)} %collective-permute-done.1), channel_id=1, source_target_pairs={{0,1},{1,0},{2,3},{3,2},{4,5},{5,4},{6,7},{7,6},{8,9},{9,8},{10,11... | collective-permute-start | bytes 1572872 | tf_op jit(solution)/shard_map/ppermute | solution.py:67
Sparse Core Ops, SparseCore 0:
  10.3 109.2 all-gather.4

commit v2 on v1

--- a/solution.py
+++ b/solution.py
@@ -1,4 +1,5 @@
 import jax
+import numpy as np
 import jax.numpy as jnp
 from jax import lax
 from jax.experimental import pallas as pl
@@ -39,7 +40,7 @@
         )
 
 
-def states_before(state, total_log, axes):
+def state_slices(state, total_log, axes):
     count = lax.axis_size(axes)
     head_count, head_width, width = state.shape
     rows = head_count * head_width // count
@@ -48,7 +49,12 @@
     factors = jnp.stack([high, low], axis=1)
     factors = jnp.repeat(factors, count // head_count, axis=0)
     factors = jnp.broadcast_to(factors[:, :, None], (count, 2, width))
-    sent = jnp.concatenate([slices, factors], axis=1)
+    return jnp.concatenate([slices, factors], axis=1)
+
+
+def states_before(sent, axes):
+    count, rows, width = sent.shape
+    rows = rows - 2
     pieces = lax.all_to_all(sent, axes, 0, 0, tiled=True)
     prior = pl.pallas_call(
         scan_kernel,
@@ -60,7 +66,47 @@
         ),
     )(pieces)
     back = lax.all_to_all(prior, axes, 0, 0, tiled=True)
-    return back.reshape(head_count, head_width, width)
+    return back.reshape(count * rows, width)
+
+
+ALL_AXES = ("section", *CTX, "mp")
+
+
+def crossed_groups(first):
+    sizes = [lax.axis_size(name) for name in ALL_AXES]
+    index = np.arange(np.prod(sizes)).reshape(sizes)
+    groups = []
+    for section in range(sizes[0]):
+        for core in range(2):
+            grid = index[section, :, :, core]
+            groups += (grid if (core == 0) == first else grid.T).tolist()
+    return groups
+
+
+def weight_part(rows):
+    count = lax.axis_size(CTX[0])
+    pieces = lax.all_to_all(
+        jnp.broadcast_to(rows[None], (count, *rows.shape)),
+        ALL_AXES,
+        0,
+        0,
+        axis_index_groups=crossed_groups(True),
+        tiled=True,
+    )
+    return pieces.reshape(count * rows.shape[0], rows.shape[1])
+
+
+def gathered_weight(part):
+    return lax.all_gather(
+        part, ALL_AXES, axis_index_groups=crossed_groups(False), axis=0, tiled=True
+    )
+
+
+def weight_order(features):
+    tokens, width = features.shape
+    outer, inner = (lax.axis_size(name) for name in CTX)
+    crossed = features.reshape(tokens, outer, inner, -1).transpose(0, 2, 1, 3)
+    return jnp.where(lax.axis_index("mp") == 0, features, crossed.reshape(tokens, width))
 
 
 def other_half(x, axis):
@@ -99,7 +145,7 @@
     norm_gain,
     next_weight,
 ):
-    full_weight = lax.all_gather(next_weight[0], CTX, axis=0, tiled=True)
+    part = weight_part(next_weight[0])
     tap_count = conv_head.shape[1]
     token_count = head_input.shape[1]
     local_width = head_input.shape[2]
@@ -145,7 +191,9 @@
     updates = jnp.einsum(
         "cshp,hcsn->chpn", blocks_x, weighted_b, preferred_element_type=jnp.float32
     )
-    prior_state = states_before(updates[0], cumulative[:, 0, -1], CTX)
+    sent = state_slices(updates[0], cumulative[:, 0, -1], CTX)
+    full_weight = gathered_weight(lax.optimization_barrier((part, sent))[0])
+    prior_state = states_before(sent, CTX).reshape(head_count, head_width, STATE)
     inter_part = (
         jnp.einsum("ctn,hpn->cthp", blocks_c, prior_state, preferred_element_type=jnp.float32)
         * jnp.exp(cumulative).transpose(1, 2, 0)[..., None]
@@ -167,7 +215,7 @@
     features = jnp.concatenate(
         [jnp.where(low, arrived, other), jnp.where(low, other, arrived)], axis=1
     )
-    result = jnp.dot(features, full_weight, preferred_element_type=jnp.float32)
+    result = jnp.dot(weight_order(features), full_weight, preferred_element_type=jnp.float32)
     return result.astype(jnp.bfloat16)[None]
 
 

time: 134 us -> 131 us (0.978)
  starting transfers between devices: 19.1 us -> 25.2 us
  blocking collectives: 35.4 us -> 30.1 us
  other arithmetic: 5.86 us -> 3.34 us
    all_gather x1, waiting for transfers between devices: 14.7 us -> 0.02 us  [gathered_weight(): lax.all_gather(part, ALL_AXES, axis_index_groups=crossed_groups(False), a...]
    all_to_all x0 -> x1, waiting for transfers between devices: none -> 13.3 us  [weight_part(): lax.all_to_all(jnp.broadcast_to(rows[None], (count, *rows.shape)), ALL_AX...]
    all_to_all x0 -> x1, starting transfers between devices: none -> 6.96 us  [weight_part(): lax.all_to_all(jnp.broadcast_to(rows[None], (count, *rows.shape)), ALL_AX...]
    all_to_all x1, blocking collectives: 30.6 us -> 23.8 us  [states_before(): pieces = lax.all_to_all(sent, axes, 0, 0, tiled=True)]
    broadcast_in_dim x2 -> x3, local copies, waits for them, and re-layouts: 0.14 us -> 2.13 us  [the longest x1 1.99 us: weight_part(): jnp.broadcast_to(rows[None], (count, *rows.shape))]
    slice x2, local copies, waits for them, and re-layouts: 1.72 us -> 0.02 us  [causal_conv(): summed = summed + weights[offset] * padded[offset:offset + length]]
    all_gather x1, blocking collectives: 4.81 us -> 6.27 us  [gathered_total(): return lax.all_gather(x, axis).sum(0)]
  transfers between devices with their start and end apart: 5 -> 6, of which waited for: 4 -> 4; matrix products, arithmetic and copies ran while one was open for 11% -> 7% of each run, Pallas kernels for 1% -> 1%
where the time goes in v2:
time: 131 us
  waiting for transfers between devices  41.1 us (31%)
  blocking collectives  30.1 us (23%)
  starting transfers between devices  25.2 us (19%)
  between operations  13.7 us (10%)
  matrix products  9.8 us (7%)
  local copies, waits for them, and re-layouts  5.69 us (4%)
  other arithmetic  3.34 us (3%)
  Pallas kernels  1.88 us (1%)
    all_to_all x1, blocking collectives, states_before(): pieces = lax.all_to_all(sent, axes, 0, 0, tiled=True)  23.8 us
    all_to_all x1, waiting for transfers between devices, weight_part(): lax.all_to_all(jnp.broadcast_to(rows[None], (count, *rows.shape)), ALL_AX...  13.3 us
    all_to_all x1, waiting for transfers between devices, states_before(): back = lax.all_to_all(prior, axes, 0, 0, tiled=True)  13.2 us
    ppermute x1, waiting for transfers between devices, shifted(): return lax.ppermute(value, axis, pairs)  13.1 us
    all_to_all x1, starting transfers between devices, states_before(): back = lax.all_to_all(prior, axes, 0, 0, tiled=True)  7.22 us
    all_to_all x1, starting transfers between devices, weight_part(): lax.all_to_all(jnp.broadcast_to(rows[None], (count, *rows.shape)), ALL_AX...  6.96 us
    dot_general x1, matrix products, shards(): jnp.dot(weight_order(features), full_weight, preferred_element_type=jnp.f...  6.7 us
    all_gather x1, blocking collectives, gathered_total(): return lax.all_gather(x, axis).sum(0)  6.27 us
  transfers between devices with their start and end apart: 6, of which 4 were waited for; matrix products, arithmetic and copies ran while one was open for 7% of the time, Pallas kernels for 1%

profile of v2, /device:TPU:1, one launch (start us, length us, event | category | flops | bytes accessed | tf_op | source)
XLA Modules:
  0.0 130.9 jit_solution(17652680666183074180)
XLA Ops:
  6.6 0.7 slice_bitcast_fusion.1
  7.3 0.7 slice_bitcast_fusion
  8.0 4.8 %collective-permute-start = (bf16[3,1280]{1,0:T(4,128)(2,1)S(1)}, bf16[3,1280]{1,0:T(4,128)(2,1)S(1)}, u32[]{:S(2)}, u32[]{:S(2)}) collective-permute-start(bf16[3,1280]{1,0:T(4,128)(2,1)S(1)} %pad_maximum_fusion.2), channel_id=1, source_target_pairs={{0,2},{2,4},{4,6},{6,8},{8,10},{10,12},{12,14},{14,16},{16,18},{18... | collective-permute-start | bytes 23048 | tf_op jit(solution)/shard_map/ppermute | solution.py:23
  12.9 2.0 %broadcast_in_dim.46 = bf16[8,32,2048]{2,1,0:T(8,128)(2,1)} broadcast(bf16[32,2048]{1,0:T(8,128)(2,1)} %bitcast.104), dimensions={1,2} | broadcast | bytes 1179648 | tf_op jit(solution)/shard_map/broadcast_in_dim | solution.py:89
  14.9 7.0 %all-to-all-start.2 = ((bf16[8,32,2048]{2,1,0:T(8,128)(2,1)}), bf16[8,32,2048]{2,1,0:T(8,128)(2,1)S(1)}, u32[]{:S(2)}, u32[]{:S(2)}) async-start(bf16[8,32,2048]{2,1,0:T(8,128)(2,1)} %broadcast_in_dim.46), calls=%async_computation.2 | async-start | bytes 2097152 | tf_op jit(solution)/shard_map/all_to_all | solution.py:88
  22.0 0.2 fusion.28
  22.2 0.3 slice_reduce_fusion
  22.6 0.2 copy.24
  23.0 0.2 copy.25
  23.2 0.3 maximum_convert_fusion
  23.6 0.1 fusion.25
  23.7 1.6 %multiply_convert_fusion.2 = bf16[256,1024]{0,1:T(8,128)(2,1)S(1)} fusion(f32[259,1024]{0,1:T(8,128)S(1)} %maximum_convert_fusion, f32[1024]{0:T(1024)S(1)} %bitcast.109, f32[1024]{0:T(1024)S(1)} %bitcast.110, f32[1024]{0:T(1024)S(1)} %bitcast.108, f32[1024]{0:T(1024)S(1)} %bitcast.107), kind=kLoop, calls=%fused_computation.38 | loop fusion | flops 3145728 | bytes 4734976 | tf_op jit(solution)/shard_map/convert_element_type | solution.py:165
  25.3 0.8 convolution_convert_fusion.1
  26.2 0.1 broadcast_in_dim.44
  26.4 13.3 %all-to-all-done.2 = bf16[8,32,2048]{2,1,0:T(8,128)(2,1)S(1)} async-done(((bf16[8,32,2048]{2,1,0:T(8,128)(2,1)}), bf16[8,32,2048]{2,1,0:T(8,128)(2,1)S(1)}, u32[]{:S(2)}, u32[]{:S(2)}) %all-to-all-start.2) | async-done | bytes 1048608 | tf_op jit(solution)/shard_map/all_to_all | solution.py:88
  39.6 1.0 copy-done
  40.6 23.8 %all_to_all.15.pieces_ref = bf16[64,18,128]{2,1,0:T(8,128)(2,1)} all-to-all(bf16[64,18,128]{2,1,0:T(8,128)(2,1)S(1)} %pad_maximum_fusion.1), channel_id=1, replica_groups=mesh['section'=4,'ctx_0'=8,'ctx_1'=8,'mp'=2] {'ctx_0','ctx_1'}, dimensions={0} | all-to-all | bytes 589824 | tf_op jit(solution)/shard_map/all_to_all | solution.py:58
  64.5 1.9 %shard_map.109 = bf16[64,16,128]{2,1,0:T(8,128)(2,1)} custom-call(bf16[64,18,128]{2,1,0:T(8,128)(2,1)} %all_to_all.15.pieces_ref), custom_call_target="tpu_custom_call" | custom-call | flops 393216 | bytes 524288 | tf_op jit(solution)/shard_map/pallas_call | solution.py:59
  66.3 7.2 %all-to-all-start.1 = ((bf16[64,16,128]{2,1,0:T(8,128)(2,1)}), bf16[64,16,128]{2,1,0:T(8,128)(2,1)S(1)}, u32[]{:S(2)}, u32[]{:S(2)}) async-start(bf16[64,16,128]{2,1,0:T(8,128)(2,1)} %shard_map.109), calls=%async_computation.1 | async-start | bytes 524288 | tf_op jit(solution)/shard_map/all_to_all | solution.py:68
  73.6 0.2 copy.27
  73.8 0.2 fusion.30
  74.0 13.2 %all-to-all-done.1 = bf16[64,16,128]{2,1,0:T(8,128)(2,1)S(1)} async-done(((bf16[64,16,128]{2,1,0:T(8,128)(2,1)}), bf16[64,16,128]{2,1,0:T(8,128)(2,1)S(1)}, u32[]{:S(2)}, u32[]{:S(2)}) %all-to-all-start.1) | async-done | bytes 262176 | tf_op jit(solution)/shard_map/all_to_all | solution.py:68
  87.2 0.3 fusion.9
  87.5 1.6 %multiply_reduce_fusion = (f32[256]{0:T(256)S(1)}, f32[1,256,16,64]{1,3,2,0:T(8,128)S(1)}) fusion(bf16[1,256,16,64]{1,3,2,0:T(8,128)(2,1)S(1)} %bitcast.100, f32[16]{0:T(128)S(1)} %bitcast.119, f32[1,256,16,64]{1,3,2,0:T(8,128)S(1)} %fusion.9, bf16[256,16,64]{0,2,1:T(8,128)(2,1)S(1)} %bitcast.101, f32[16,256]{1,0:T(8,128)S(1)} %compare_select_fusion, ...), kind=kOutput, calls=%fused_computation.35 | convolution fusion | flops 143654656 | bytes 4031552 | tf_op jit(solution)/shard_map/hcts,cshp->cthp/dot_general | solution.py:186
  89.1 6.3 %all-gather.1 = f32[2,1,256]{2,1,0:T(1,128)S(1)} all-gather(f32[1,1,256]{2,1,0:T(1,128)S(1)} %bitcast.118), channel_id=2, replica_groups=mesh['section'=4,'ctx_0'=8,'ctx_1'=8,'mp'=2] {'mp'}, dimensions={0}, use_global_device_ids=true | all-gather | bytes 3072 | tf_op jit(solution)/shard_map/all_gather | solution.py:117
  95.4 0.4 fusion.23
  95.8 3.1 %collective-permute-start.1 = (bf16[256,1024]{0,1:T(8,128)(2,1)S(1)}, bf16[256,1024]{0,1:T(8,128)(2,1)S(1)}, u32[]{:S(2)}, u32[]{:S(2)}) collective-permute-start(bf16[256,1024]{0,1:T(8,128)(2,1)S(1)} %fusion.23), channel_id=1, source_target_pairs={{0,128},{128,256},{256,384},{384,0},{1,129},{129,257},{257,385},{3... | collective-permute-start | bytes 1572872 | tf_op jit(solution)/shard_map/ppermute | solution.py:123
  99.0 13.1 %collective-permute-done.1 = bf16[256,1024]{0,1:T(8,128)(2,1)S(1)} collective-permute-done((bf16[256,1024]{0,1:T(8,128)(2,1)S(1)}, bf16[256,1024]{0,1:T(8,128)(2,1)S(1)}, u32[]{:S(2)}, u32[]{:S(2)}) %collective-permute-start.1) | collective-permute-done | bytes 524320 | tf_op jit(solution)/shard_map/ppermute | solution.py:123
  112.1 3.1 %collective-permute-start.2 = (bf16[256,1024]{0,1:T(8,128)(2,1)S(1)}, bf16[256,1024]{0,1:T(8,128)(2,1)S(1)}, u32[]{:S(2)}, u32[]{:S(2)}) collective-permute-start(bf16[256,1024]{0,1:T(8,128)(2,1)S(1)} %collective-permute-done.1), channel_id=1, source_target_pairs={{0,1},{1,0},{2,3},{3,2},{4,5},{5,4},{6,7},{7,6},{8,9},{9,8},{10,11... | collective-permute-start | bytes 1572872 | tf_op jit(solution)/shard_map/ppermute | solution.py:113
  115.2 1.5 %collective-permute-done.2 = bf16[256,1024]{0,1:T(8,128)(2,1)S(1)} collective-permute-done((bf16[256,1024]{0,1:T(8,128)(2,1)S(1)}, bf16[256,1024]{0,1:T(8,128)(2,1)S(1)}, u32[]{:S(2)}, u32[]{:S(2)}) %collective-permute-start.2) | collective-permute-done | bytes 524320 | tf_op jit(solution)/shard_map/ppermute | solution.py:113
  116.9 0.4 bitcast_select_fusion
  117.4 6.7 %fusion = bf16[1,256,2048]{2,1,0:T(8,128)(2,1)} fusion(bf16[256,2048]{0,1:T(8,128)(2,1)S(1)} %bitcast_select_fusion, bf16[2048,2048]{1,0:T(8,128)(2,1)} %all-gather.4.cloned.1.call-done), kind=kOutput, calls=%fused_computation.2 | convolution fusion | flops 2148007936 | bytes 10485760 | tf_op jit(solution)/shard_map/dot_general | solution.py:218
  (46 shorter events, 0.8 us)
Async XLA Ops:
  6.5 16.1 %copy-start.1 = (bf16[1,256,1024]{2,1,0:T(8,128)(2,1)S(1)}, bf16[1,256,1024]{2,1,0:T(8,128)(2,1)}, u32[]{:S(2)}) copy-start(bf16[1,256,1024]{2,1,0:T(8,128)(2,1)} %param.11) | copy-start | bytes 1572868
  6.5 15.3 %copy-start.9 = (f32[1,16]{1,0:T(1,128)S(1)}, f32[1,16]{1,0:T(1,128)}, u32[]{:S(2)}) copy-start(f32[1,16]{1,0:T(1,128)} %param.16) | copy-start | bytes 196
  6.5 15.3 %copy-start.7 = (f32[1,4,256]{2,1,0:T(4,128)S(1)}, f32[1,4,256]{2,1,0:T(4,128)}, u32[]{:S(2)}) copy-start(f32[1,4,256]{2,1,0:T(4,128)} %param.19) | copy-start | bytes 12292
  6.5 15.4 %copy-start.4 = (f32[1,16,256]{2,1,0:T(8,128)S(1)}, f32[1,16,256]{2,1,0:T(8,128)}, u32[]{:S(2)}) copy-start(f32[1,16,256]{2,1,0:T(8,128)} %param.14) | copy-start | bytes 49156
  6.5 15.4 %copy-start.8 = (f32[1,16]{1,0:T(1,128)S(1)}, f32[1,16]{1,0:T(1,128)}, u32[]{:S(2)}) copy-start(f32[1,16]{1,0:T(1,128)} %param.15) | copy-start | bytes 196
  6.5 15.9 %copy-start.5 = (f32[1,4,1024]{2,1,0:T(4,128)S(1)}, f32[1,4,1024]{2,1,0:T(4,128)}, u32[]{:S(2)}) copy-start(f32[1,4,1024]{2,1,0:T(4,128)} %param.18) | copy-start | bytes 49156
  8.0 14.9 %collective-permute-start = (bf16[3,1280]{1,0:T(4,128)(2,1)S(1)}, bf16[3,1280]{1,0:T(4,128)(2,1)S(1)}, u32[]{:S(2)}, u32[]{:S(2)}) collective-permute-start(bf16[3,1280]{1,0:T(4,128)(2,1)S(1)} %pad_maximum_fusion.2), channel_id=1, source_target_pairs={{0,2},{2,4},{4,6},{6,8},{8,10},{10,12},{12,14},{14,16},{16,18},{18... | collective-permute-start | bytes 23048 | tf_op jit(solution)/shard_map/ppermute | solution.py:23
  14.9 8.3 %copy-start.3 = (bf16[1,256,256]{2,1,0:T(8,128)(2,1)S(1)}, bf16[1,256,256]{2,1,0:T(8,128)(2,1)}, u32[]{:S(2)}) copy-start(bf16[1,256,256]{2,1,0:T(8,128)(2,1)} %param.12) | copy-start | bytes 393220
  14.9 24.8 %all-to-all-start.2 = ((bf16[8,32,2048]{2,1,0:T(8,128)(2,1)}), bf16[8,32,2048]{2,1,0:T(8,128)(2,1)S(1)}, u32[]{:S(2)}, u32[]{:S(2)}) async-start(bf16[8,32,2048]{2,1,0:T(8,128)(2,1)} %broadcast_in_dim.46), calls=%async_computation.2 | async-start | bytes 2097152 | tf_op jit(solution)/shard_map/all_to_all | solution.py:88
  21.8 95.5 %all-gather.4.cloned.1.call-start = ((), (), s32[]{:S(2)}) async-start(), calls=%async_computation.3 | async-start | bytes 9437184 | tf_op jit(solution)/shard_map/all_gather | solution.py:100
  26.1 47.4 %copy-start.2 = (bf16[1,256,1024]{2,1,0:T(8,128)(2,1)S(1)}, bf16[1,256,1024]{2,1,0:T(8,128)(2,1)}, u32[]{:S(2)}) copy-start(bf16[1,256,1024]{2,1,0:T(8,128)(2,1)} %param.13) | copy-start | bytes 1572868
  39.6 1.0 copy-start
  64.4 23.0 %copy-start.10 = (f32[1,16]{1,0:T(1,128)S(1)}, f32[1,16]{1,0:T(1,128)}, u32[]{:S(2)}) copy-start(f32[1,16]{1,0:T(1,128)} %param.17) | copy-start | bytes 196
  66.3 20.9 %all-to-all-start.1 = ((bf16[64,16,128]{2,1,0:T(8,128)(2,1)}), bf16[64,16,128]{2,1,0:T(8,128)(2,1)S(1)}, u32[]{:S(2)}, u32[]{:S(2)}) async-start(bf16[64,16,128]{2,1,0:T(8,128)(2,1)} %shard_map.109), calls=%async_computation.1 | async-start | bytes 524288 | tf_op jit(solution)/shard_map/all_to_all | solution.py:68
  87.5 7.9 %copy-start.6 = (f32[1,1024]{1,0:T(1,128)S(1)}, f32[1,1024]{1,0:T(1,128)}, u32[]{:S(2)}) copy-start(f32[1,1024]{1,0:T(1,128)} %param.20) | copy-start | bytes 12292
  95.8 16.2 %collective-permute-start.1 = (bf16[256,1024]{0,1:T(8,128)(2,1)S(1)}, bf16[256,1024]{0,1:T(8,128)(2,1)S(1)}, u32[]{:S(2)}, u32[]{:S(2)}) collective-permute-start(bf16[256,1024]{0,1:T(8,128)(2,1)S(1)} %fusion.23), channel_id=1, source_target_pairs={{0,128},{128,256},{256,384},{384,0},{1,129},{129,257},{257,385},{3... | collective-permute-start | bytes 1572872 | tf_op jit(solution)/shard_map/ppermute | solution.py:123
  112.1 4.6 %collective-permute-start.2 = (bf16[256,1024]{0,1:T(8,128)(2,1)S(1)}, bf16[256,1024]{0,1:T(8,128)(2,1)S(1)}, u32[]{:S(2)}, u32[]{:S(2)}) collective-permute-start(bf16[256,1024]{0,1:T(8,128)(2,1)S(1)} %collective-permute-done.1), channel_id=1, source_target_pairs={{0,1},{1,0},{2,3},{3,2},{4,5},{5,4},{6,7},{7,6},{8,9},{9,8},{10,11... | collective-permute-start | bytes 1572872 | tf_op jit(solution)/shard_map/ppermute | solution.py:113
Sparse Core Ops, SparseCore 0:
  40.7 69.5 all-gather.3

commit v3 on v2

v3 whole, which is shorter than its diff:
```python
import jax
import numpy as np
import jax.numpy as jnp
from jax import lax
from jax.experimental import pallas as pl
from jax.experimental.pallas import tpu as pltpu
from jax.sharding import Mesh
from jax.sharding import PartitionSpec as P

STATE = 128
BLOCK = 256
FEATURES = 2048
CTX = ("ctx_0", "ctx_1")
CTX_SIDE = 8
EXTRA = 8
TAIL = 8


NORM_FLOOR = 0.25


def small_vmem(mebibytes):
    return pltpu.CompilerParams(vmem_limit_bytes=mebibytes * 2**20)


HIGHEST = lax.Precision.HIGHEST


def from_behind(value, axis, steps):
    count = lax.axis_size(axis)
    first, last = (max(0, -steps), min(count, count - steps))
    return lax.ppermute(value, axis, [(source, source + steps) for source in range(first, last)])


def split_in_two(x):
    high = lax.reduce_precision(x, 8, 7)
    return high.astype(jnp.bfloat16), (x - high).astype(jnp.bfloat16)


def scan_kernel(pieces_ref, prior_ref):
    count, _, width = pieces_ref.shape
    rows = prior_ref.shape[1]
    carried = jnp.zeros((rows, width), jnp.float32)
    for k in range(count):
        prior_ref[k] = carried.astype(jnp.bfloat16)
        factor = pieces_ref[k, rows : rows + 2, :].astype(jnp.float32)
        carried = (factor[0:1] + factor[1:2]) * carried + pieces_ref[k, 0:rows, :].astype(
            jnp.float32
        )


def states_before(sent, axes):
    count, rows, width = sent.shape
    rows = rows - EXTRA
    pieces = lax.all_to_all(sent, axes, 0, 0, tiled=True)
    prior = pl.pallas_call(
        scan_kernel,
        out_shape=jax.ShapeDtypeStruct((count, rows, width), jnp.bfloat16),
        in_specs=[pl.BlockSpec(memory_space=pltpu.VMEM)],
        out_specs=pl.BlockSpec(memory_space=pltpu.VMEM),
        compiler_params=small_vmem(4),
        cost_estimate=pl.CostEstimate(
            flops=3 * count * rows * width, bytes_accessed=4 * count * rows * width, transcendentals=0
        ),
    )(pieces)
    back = lax.all_to_all(prior, axes, 0, 0, tiled=True)
    return back.reshape(count * rows, width)


ALL_AXES = ("section", *CTX, "mp")


def crossed_groups(first):
    sizes = [lax.axis_size(name) for name in ALL_AXES]
    index = np.arange(np.prod(sizes)).reshape(sizes)
    groups = []
    for section in range(sizes[0]):
        for core in range(2):
            grid = index[section, :, :, core]
            groups += (grid if (core == 0) == first else grid.T).tolist()
    return groups


def tail_kernel(wide_ref, narrow_ref, tail_ref):
    width = wide_ref.shape[1]
    tail_ref[:, :width] = wide_ref[...]
    tail_ref[:, width:] = narrow_ref[...]


def last_positions(wide, narrow):
    last = wide.shape[0] // TAIL - 1
    width = wide.shape[1] + narrow.shape[1]
    return pl.pallas_call(
        tail_kernel,
        out_shape=jax.ShapeDtypeStruct((TAIL, width), wide.dtype),
        grid=(1,),
        in_specs=[
            pl.BlockSpec((TAIL, wide.shape[1]), lambda i: (last, 0)),
            pl.BlockSpec((TAIL, narrow.shape[1]), lambda i: (last, 0)),
        ],
        out_specs=pl.BlockSpec((TAIL, width), lambda i: (0, 0)),
        cost_estimate=pl.CostEstimate(flops=0, bytes_accessed=4 * TAIL * width, transcendentals=0),
    )(wide, narrow)


def copies_kernel(rows_ref, copies_ref):
    rows = rows_ref[...]
    for k in range(copies_ref.shape[0]):
        copies_ref[k] = rows


def copied(rows):
    count = lax.axis_size(CTX[0])
    vmem = pl.BlockSpec(memory_space=pltpu.VMEM)
    return pl.pallas_call(
        copies_kernel,
        out_shape=jax.ShapeDtypeStruct((count, *rows.shape), rows.dtype),
        in_specs=[vmem],
        out_specs=vmem,
        compiler_params=small_vmem(4),
        cost_estimate=pl.CostEstimate(
            flops=0, bytes_accessed=2 * (count + 1) * rows.size, transcendentals=0
        ),
    )(rows)


def weight_part(copies):
    pieces = lax.all_to_all(
        copies, ALL_AXES, 0, 0, axis_index_groups=crossed_groups(True), tiled=True
    )
    return pieces.reshape(-1, copies.shape[2])


def prepare_kernel(
    wide_ref,
    narrow_ref,
    behind_ref,
    wide_taps_ref,
    narrow_taps_ref,
    tail_weight_ref,
    factors_ref,
    wide_out_ref,
    narrow_out_ref,
    sent_ref,
    padded_ref,
    weighted_ref,
):
    tokens, width = wide_ref.shape
    heads = tail_weight_ref.shape[0]
    head_width = width // heads
    lanes = 128
    taps = wide_taps_ref.shape[0]
    first = TAIL - taps + 1

    def summed(source_ref, start, behind_start, taps_ref):
        padded_ref[0:TAIL, :] = behind_ref[:, behind_start : behind_start + lanes].astype(
            jnp.float32
        )
        padded_ref[TAIL:, :] = source_ref[:, start : start + lanes].astype(jnp.float32)
        total = jnp.zeros((tokens, lanes), jnp.float32)
        for tap in range(taps):
            total = total + taps_ref[tap : tap + 1, start : start + lanes] * (
                padded_ref[first + tap : first + tap + tokens, :]
            )
        return total

    for start in range(0, narrow_ref.shape[1], lanes):
        narrow_out_ref[:, start : start + lanes] = summed(
            narrow_ref, start, width + start, narrow_taps_ref
        ).astype(jnp.bfloat16)
    for start in range(0, width, lanes):
        active = jax.nn.silu(summed(wide_ref, start, start, wide_taps_ref)).astype(jnp.bfloat16)
        turned = active.astype(jnp.float32).T
        wide_out_ref[start : start + lanes, :] = turned.astype(jnp.bfloat16)
        for part in range(0, lanes, head_width):
            head = (start + part) // head_width
            weighted_ref[start + part : start + part + head_width, :] = (
                turned[part : part + head_width, :] * tail_weight_ref[head : head + 1, :]
            ).astype(jnp.bfloat16)
    state = jnp.dot(
        weighted_ref[...], narrow_out_ref[:, :STATE], preferred_element_type=jnp.float32
    )
    count, _, state_width = sent_ref.shape
    rows = width // count
    sent_ref[:, 0:rows, :] = state.astype(jnp.bfloat16).reshape(count, rows, state_width)
    for k in range(count):
        sent_ref[k, rows:, :] = factors_ref[k * heads // count]


def prepared(wide, narrow, behind, wide_taps, narrow_taps, tail_weight, total_log, axes):
    count = lax.axis_size(axes)
    tokens, width = wide.shape
    high, low = split_in_two(jnp.exp(total_log))
    factors = jnp.stack([high, low] + [jnp.zeros_like(high)] * (EXTRA - 2), axis=1)
    factors = jnp.broadcast_to(factors[:, :, None], (*factors.shape, STATE))
    vmem = pl.BlockSpec(memory_space=pltpu.VMEM)
    return pl.pallas_call(
        prepare_kernel,
        out_shape=(
            jax.ShapeDtypeStruct((width, tokens), jnp.bfloat16),
            jax.ShapeDtypeStruct(narrow.shape, jnp.bfloat16),
            jax.ShapeDtypeStruct((count, width // count + EXTRA, STATE), jnp.bfloat16),
        ),
        in_specs=[vmem] * 7,
        out_specs=(vmem, vmem, vmem),
        scratch_shapes=[
            pltpu.VMEM((TAIL + tokens, 128), jnp.float32),
            pltpu.VMEM((width, tokens), jnp.bfloat16),
        ],
        compiler_params=small_vmem(12),
    cost_estimate=pl.CostEstimate(
        flops=2 * tokens * width * STATE,
        bytes_accessed=8 * tokens * width,
        transcendentals=tokens * width,
    ),
    )(wide, narrow, behind, wide_taps, narrow_taps, tail_weight, factors)


def gathered_weight(part):
    return lax.all_gather(
        part, ALL_AXES, axis_index_groups=crossed_groups(False), axis=0, tiled=True
    )


def assemble_kernel(core_ref, own_ref, other_ref, features_ref, scale_ref, rows_ref):
    half = own_ref.shape[0] - EXTRA
    tokens = own_ref.shape[1]
    ring = CTX_SIDE
    block = half * 2 // (ring * ring)

    @pl.when(core_ref[0] == 0)
    def _():
        rows_ref[0:half, :] = own_ref[0:half, :]
        rows_ref[half : 2 * half, :] = other_ref[0:half, :]

    @pl.when(core_ref[0] != 0)
    def _():
        for outer in range(ring):
            source = other_ref if outer < ring // 2 else own_ref
            for inner in range(ring):
                start = ((outer % (ring // 2)) * ring + inner) * block
                target = (inner * ring + outer) * block
                rows_ref[target : target + block, :] = source[start : start + block, :]

    for start in range(0, 2 * half, tokens):
        part = rows_ref[start : start + tokens, :].astype(jnp.float32)
        features_ref[:, start : start + tokens] = part.T.astype(jnp.bfloat16)
    squares = jnp.sum(
        own_ref[half : half + EXTRA, :].astype(jnp.float32)
        + other_ref[half : half + EXTRA, :].astype(jnp.float32),
        axis=0,
        keepdims=True,
    )
    scale = lax.rsqrt(squares / FEATURES + NORM_FLOOR)
    scale_ref[...] = jnp.broadcast_to(scale, (scale_ref.shape[1], tokens)).T


def assembled(own, other, axis):
    tokens = own.shape[1]
    width = 2 * (own.shape[0] - EXTRA)
    core = lax.axis_index(axis).astype(jnp.int32).reshape(1)
    vmem = pl.BlockSpec(memory_space=pltpu.VMEM)
    return pl.pallas_call(
        assemble_kernel,
        out_shape=(
            jax.ShapeDtypeStruct((tokens, width), jnp.bfloat16),
            jax.ShapeDtypeStruct((tokens, 128), jnp.float32),
        ),
        in_specs=[pl.BlockSpec(memory_space=pltpu.SMEM), vmem, vmem],
        out_specs=(vmem, vmem),
        scratch_shapes=[pltpu.VMEM((width, tokens), jnp.bfloat16)],
        compiler_params=small_vmem(12),
        cost_estimate=pl.CostEstimate(
            flops=4 * tokens * width, bytes_accessed=4 * tokens * width, transcendentals=0
        ),
    )(core, own, other)


def project_kernel(features_ref, scale_ref, weight_ref, out_ref, rows_ref, total_ref, arrived):
    depth, width = rows_ref.shape
    steps = arrived.shape[0]
    block = depth // steps
    part_width = 512

    def fetch(step):
        rows = pl.ds(step * block, block)
        return pltpu.make_async_copy(weight_ref.at[rows], rows_ref.at[rows], arrived.at[step])

    for step in range(steps):
        fetch(step).start()
    for step in range(steps):
        fetch(step).wait()
        for start in range(0, width, part_width):
            columns = slice(start, start + part_width)
            product = jnp.dot(
                features_ref[:, step * block : (step + 1) * block],
                rows_ref[step * block : (step + 1) * block, columns],
                preferred_element_type=jnp.float32,
            )
            if step > 0:
                product = total_ref[:, columns] + product
            if step < steps - 1:
                total_ref[:, columns] = product
            else:
                out_ref[:, columns] = (product * scale_ref[:, 0:1]).astype(out_ref.dtype)


def projected(features, scale, weight, steps=8):
    tokens, depth = features.shape
    width = weight.shape[1]
    vmem = pl.BlockSpec(memory_space=pltpu.VMEM)
    return pl.pallas_call(
        project_kernel,
        out_shape=jax.ShapeDtypeStruct((tokens, width), jnp.bfloat16),
        in_specs=[vmem, vmem, pl.BlockSpec(memory_space=pl.ANY)],
        out_specs=vmem,
        scratch_shapes=[
            pltpu.VMEM((depth, width), weight.dtype),
            pltpu.VMEM((tokens, width), jnp.float32),
            pltpu.SemaphoreType.DMA((steps,)),
        ],
        compiler_params=small_vmem(52),
        cost_estimate=pl.CostEstimate(
            flops=2 * tokens * depth * width, bytes_accessed=2 * depth * width, transcendentals=0
        ),
    )(features, scale, weight)


def other_half(x, axis):
    return lax.ppermute(x, axis, [(0, 1), (1, 0)])


def shifted(value, axis, steps):
    count = lax.axis_size(axis)
    pairs = [(source, (source + steps) % count) for source in range(count)]
    return lax.ppermute(value, axis, pairs)


def section_block(
    head_input,
    state_proj,
    gate_input,
    step_raw,
    step_bias,
    decay_log,
    skip_gain,
    conv_head,
    conv_state,
    norm_gain,
    next_weight,
):
    token_count = head_input.shape[1]
    local_width = head_input.shape[2]
    head_count = step_raw.shape[1]
    head_width = local_width // head_count
    block_count = token_count // BLOCK
    part = weight_part(copied(next_weight[0]))
    tails = last_positions(head_input[0], state_proj[0])
    behind = from_behind(tails, CTX, 1)
    step_size = jax.nn.softplus(step_raw[0] + step_bias[0][:, None])
    log_decay = -jnp.exp(decay_log[0])[:, None] * step_size
    blocks_step = step_size.reshape(head_count, block_count, BLOCK)
    blocks_decay = log_decay.reshape(head_count, block_count, BLOCK)
    row_index = lax.broadcasted_iota(jnp.int32, (BLOCK, BLOCK), 0)
    col_index = lax.broadcasted_iota(jnp.int32, (BLOCK, BLOCK), 1)
    causal_mask = row_index >= col_index
    lower_tri = causal_mask.astype(jnp.float32)
    cumulative = jnp.einsum("hcs,ts->hct", blocks_decay, lower_tri, precision=HIGHEST)
    tail_weight = jnp.exp(cumulative[..., -1:] - cumulative) * blocks_step
    conv_xt, conv_bc, sent = prepared(
        head_input[0],
        state_proj[0],
        behind,
        conv_head[0],
        conv_state[0],
        tail_weight[:, 0],
        cumulative[:, 0, -1],
        CTX,
    )
    blocks_x = conv_xt.T.reshape(block_count, BLOCK, head_count, head_width)
    blocks_b = conv_bc[:, :STATE].reshape(block_count, BLOCK, STATE)
    blocks_c = conv_bc[:, STATE:].reshape(block_count, BLOCK, STATE)
    scores = jnp.einsum("ctn,csn->cts", blocks_c, blocks_b, preferred_element_type=jnp.float32)
    decay_diff = jnp.where(causal_mask, cumulative[..., :, None] - cumulative[..., None, :], 0.0)
    mix_weight = jnp.where(
        causal_mask, scores[None] * jnp.exp(decay_diff) * blocks_step[:, :, None, :], 0.0
    ).astype(jnp.bfloat16)
    intra_part = jnp.einsum(
        "hcts,cshp->cthp", mix_weight, blocks_x, preferred_element_type=jnp.float32
    )
    full_weight = gathered_weight(part)
    prior_state = states_before(sent, CTX).reshape(head_count, head_width, STATE)
    inter_part = (
        jnp.einsum("ctn,hpn->cthp", blocks_c, prior_state, preferred_element_type=jnp.float32)
        * jnp.exp(cumulative).transpose(1, 2, 0)[..., None]
    )
    output = (
        intra_part + inter_part + skip_gain[0][None, None, :, None] * blocks_x.astype(jnp.float32)
    )
    gated = output.reshape(token_count, local_width) * jax.nn.silu(
        gate_input[0].astype(jnp.float32)
    )
    high, low = split_in_two(jnp.sum(gated * gated, axis=1))
    extra = jnp.stack([high, low] + [jnp.zeros_like(high)] * (EXTRA - 2), axis=1)
    features = (gated * norm_gain[0][None]).astype(jnp.bfloat16)
    arrived = shifted(jnp.concatenate([features, extra], axis=1), "section", 1)
    other = other_half(arrived, "mp")
    features, scale = assembled(arrived.T, other.T, "mp")
    return projected(features, scale, full_weight)[None]


def solution(mesh):
    finer = Mesh(
        mesh.devices.reshape(mesh.shape["section"], 8, 8, mesh.shape["mp"]),
        ("section", "ctx_0", "ctx_1", "mp"),
    )
    in_specs = (
        P("section", CTX, "mp"),
        P("section", CTX, None),
        P("section", CTX, "mp"),
        P("section", "mp", CTX),
        P("section", "mp"),
        P("section", "mp"),
        P("section", "mp"),
        P("section", None, "mp"),
        P("section", None, None),
        P("section", "mp"),
        P("section", CTX, "mp"),
    )
    out_specs = P("section", CTX, "mp")
    return jax.shard_map(
        section_block, mesh=finer, in_specs=in_specs, out_specs=out_specs, check_vma=False
    )
```

time: 131 us -> 126 us (0.962)
  blocking collectives: 30.1 us -> 52.5 us
  waiting for transfers between devices: 41.1 us -> 23.2 us
  matrix products: 9.8 us -> 2.33 us
  Pallas kernels: 1.88 us -> 8.72 us
  local copies, waits for them, and re-layouts: 5.69 us -> 2.09 us
  starting transfers between devices: 25.2 us -> 22.5 us
  other arithmetic: 3.34 us -> 0.69 us
    all_to_all x0 -> x1, blocking collectives: none -> 25.4 us  [weight_part(): lax.all_to_all(copies, ALL_AXES, 0, 0, axis_index_groups=crossed_groups(T...]
    all_to_all x1 -> x0, waiting for transfers between devices: 13.3 us -> none  [weight_part(): lax.all_to_all(jnp.broadcast_to(rows[None], (count, *rows.shape)), ALL_AX...]
    pallas_call x0 -> x5, Pallas kernels: none -> 7.88 us  [the longest x1 4.99 us: projected(): pl.pallas_call(project_kernel, out_shape=jax.ShapeDtypeStruct((tokens, wi...]
    dot_general x6 -> x4, matrix products: 9.8 us -> 2.33 us  [the longest x1 1.67 us: section_block(): jnp.einsum('hcts,cshp->cthp', mix_weight, blocks_x, preferred_element_typ...]
    all_to_all x1 -> x0, starting transfers between devices: 6.96 us -> none  [weight_part(): lax.all_to_all(jnp.broadcast_to(rows[None], (count, *rows.shape)), ALL_AX...]
    ppermute x1, starting transfers between devices: 3.1 us -> 10 us  [other_half(): return lax.ppermute(x, axis, [(0, 1), (1, 0)])]
    all_gather x1 -> x0, blocking collectives: 6.27 us -> none  [gathered_total(): return lax.all_gather(x, axis).sum(0)]
    ppermute x1, waiting for transfers between devices: 13.1 us -> 8.45 us  [shifted(): return lax.ppermute(value, axis, pairs)]
  transfers between devices with their start and end apart: 6 -> 5, of which waited for: 4 -> 3; matrix products, arithmetic and copies ran while one was open for 7% -> 3% of each run, Pallas kernels for 1% -> 3%
where the time goes in v3:
time: 126 us
  blocking collectives  52.5 us (42%)
  waiting for transfers between devices  23.2 us (18%)
  starting transfers between devices  22.5 us (18%)
  between operations  13.7 us (11%)
  Pallas kernels  8.72 us (7%)
  matrix products  2.33 us (2%)
  local copies, waits for them, and re-layouts  2.09 us (2%)
    all_to_all x1, blocking collectives, states_before(): pieces = lax.all_to_all(sent, axes, 0, 0, tiled=True)  27 us
    all_to_all x1, blocking collectives, weight_part(): lax.all_to_all(copies, ALL_AXES, 0, 0, axis_index_groups=crossed_groups(T...  25.4 us
    all_to_all x1, waiting for transfers between devices, states_before(): back = lax.all_to_all(prior, axes, 0, 0, tiled=True)  13.2 us
    ppermute x1, starting transfers between devices, other_half(): return lax.ppermute(x, axis, [(0, 1), (1, 0)])  10 us
    ppermute x1, waiting for transfers between devices, shifted(): return lax.ppermute(value, axis, pairs)  8.45 us
    all_to_all x1, starting transfers between devices, states_before(): back = lax.all_to_all(prior, axes, 0, 0, tiled=True)  5.41 us
    pallas_call x1, Pallas kernels, projected(): pl.pallas_call(project_kernel, out_shape=jax.ShapeDtypeStruct((tokens, wi...  4.99 us
    ppermute x1, starting transfers between devices, from_behind(): lax.ppermute(value, axis, [(source, source + steps) for source in range(f...  3.98 us
  transfers between devices with their start and end apart: 5, of which 3 were waited for; matrix products, arithmetic and copies ran while one was open for 3% of the time, Pallas kernels for 3%

profile of v3, /device:TPU:1, one launch (start us, length us, event | category | flops | bytes accessed | tf_op | source)
XLA Modules:
  0.0 125.7 jit_solution(4861390159484429713)
XLA Ops:
  6.5 1.0 copy-done.2
  7.5 0.1 shard_map.113
  7.6 25.4 %all_to_all.15 = bf16[8,32,2048]{2,1,0:T(8,128)(2,1)} all-to-all(bf16[8,32,2048]{2,1,0:T(8,128)(2,1)S(1)} %shard_map.113), channel_id=1, replica_groups={{0,2,4,6,8,10,12,14},{16,18,20,22,24,26,28,30},{32,34,36,38,40,42,44,46..., dimensions={0} | all-to-all | bytes 2097152 | tf_op jit(solution)/shard_map/all_to_all | solution.py:128
  33.1 1.3 %shard_map.109 = bf16[8,1280]{1,0:T(8,128)(2,1)} custom-call(bf16[256,1024]{1,0:T(8,128)(2,1)} %bitcast.77, bf16[256,256]{1,0:T(8,128)(2,1)} %bitcast.81), custom_call_target="tpu_custom_call" | custom-call | bytes 40960 | tf_op jit(solution)/shard_map/pallas_call | solution.py:93
  34.4 4.0 %collective-permute-start = (bf16[8,1280]{1,0:T(8,128)(2,1)}, bf16[8,1280]{1,0:T(8,128)(2,1)S(1)}, u32[]{:S(2)}, u32[]{:S(2)}) collective-permute-start(bf16[8,1280]{1,0:T(8,128)(2,1)} %shard_map.109), channel_id=1, source_target_pairs={{0,2},{2,4},{4,6},{6,8},{8,10},{10,12},{12,14},{14,16},{16,18},{18... | collective-permute-start | bytes 61448 | tf_op jit(solution)/shard_map/ppermute | solution.py:32
  38.4 0.1 pad.3.clone
  38.5 0.1 pad.2.clone
  38.6 0.1 compare_select_fusion
  38.7 0.2 fusion.17
  38.9 0.3 exponential_reduce_fusion
  39.2 0.1 copy.15
  39.3 0.1 copy.16
  39.3 0.1 exponential_bitcast_fusion
  39.5 0.1 maximum_maximum_fusion
  39.5 0.1 broadcast_in_dim.26.factors_ref
  39.7 1.1 shard_map.110
  40.7 27.0 %all_to_all.16.pieces_ref = bf16[64,24,128]{2,1,0:T(8,128)(2,1)S(1)} all-to-all(bf16[64,24,128]{2,1,0:T(8,128)(2,1)S(1)} %get-tuple-element.12), channel_id=1, replica_groups=mesh['section'=4,'ctx_0'=8,'ctx_1'=8,'mp'=2] {'ctx_0','ctx_1'}, dimensions={0} | all-to-all | bytes 786432 | tf_op jit(solution)/shard_map/all_to_all | solution.py:55
  67.8 0.8 shard_map.111
  68.6 5.4 %all-to-all-start.1 = ((bf16[64,16,128]{2,1,0:T(8,128)(2,1)}), bf16[64,16,128]{2,1,0:T(8,128)(2,1)S(1)}, u32[]{:S(2)}, u32[]{:S(2)}) async-start(bf16[64,16,128]{2,1,0:T(8,128)(2,1)} %shard_map.111), calls=%async_computation.1 | async-start | bytes 524288 | tf_op jit(solution)/shard_map/all_to_all | solution.py:66
  74.0 0.2 copy.17
  74.3 0.2 fusion.19
  74.5 13.2 %all-to-all-done.1 = bf16[64,16,128]{2,1,0:T(8,128)(2,1)S(1)} async-done(((bf16[64,16,128]{2,1,0:T(8,128)(2,1)}), bf16[64,16,128]{2,1,0:T(8,128)(2,1)S(1)}, u32[]{:S(2)}, u32[]{:S(2)}) %all-to-all-start.1) | async-done | bytes 262176 | tf_op jit(solution)/shard_map/all_to_all | solution.py:66
  87.6 0.3 fusion.8
  88.0 1.7 %multiply_reduce_fusion = (f32[256]{0:T(256)S(1)}, f32[1,256,16,64]{1,3,2,0:T(8,128)S(1)}) fusion(bf16[1,256,16,64]{1,3,2,0:T(8,128)(2,1)S(1)} %bitcast.86, f32[16]{0:T(128)S(1)} %bitcast.96, f32[1,256,16,64]{1,3,2,0:T(8,128)S(1)} %fusion.8, bf16[256,16,64]{0,2,1:T(8,128)(2,1)S(1)} %bitcast.87, f32[16,256]{1,0:T(8,128)S(1)} %compare_select_fusion, ...), kind=kOutput, calls=%fused_computation.21 | convolution fusion | flops 143654656 | bytes 4031552 | tf_op jit(solution)/shard_map/hcts,cshp->cthp/dot_general | solution.py:388
  89.6 0.4 fusion.16
  90.1 0.2 concatenate.11
  90.2 3.1 %collective-permute-start.1 = (bf16[256,1032]{0,1:T(8,128)(2,1)S(1)}, bf16[256,1032]{0,1:T(8,128)(2,1)S(1)}, u32[]{:S(2)}, u32[]{:S(2)}) collective-permute-start(bf16[256,1032]{0,1:T(8,128)(2,1)S(1)} %concatenate.11), channel_id=1, source_target_pairs={{0,128},{128,256},{256,384},{384,0},{1,129},{129,257},{257,385},{3... | collective-permute-start | bytes 1585160 | tf_op jit(solution)/shard_map/ppermute | solution.py:336
  93.4 8.5 %collective-permute-done.1 = bf16[256,1032]{0,1:T(8,128)(2,1)S(1)} collective-permute-done((bf16[256,1032]{0,1:T(8,128)(2,1)S(1)}, bf16[256,1032]{0,1:T(8,128)(2,1)S(1)}, u32[]{:S(2)}, u32[]{:S(2)}) %collective-permute-start.1) | collective-permute-done | bytes 528416 | tf_op jit(solution)/shard_map/ppermute | solution.py:336
  101.8 10.0 %collective-permute-start.2 = (bf16[256,1032]{0,1:T(8,128)(2,1)S(1)}, bf16[256,1032]{0,1:T(8,128)(2,1)S(1)}, u32[]{:S(2)}, u32[]{:S(2)}) collective-permute-start(bf16[256,1032]{0,1:T(8,128)(2,1)S(1)} %collective-permute-done.1), channel_id=1, source_target_pairs={{0,1},{1,0},{2,3},{3,2},{4,5},{5,4},{6,7},{7,6},{8,9},{9,8},{10,11... | collective-permute-start | bytes 1585160 | tf_op jit(solution)/shard_map/ppermute | solution.py:330
  111.8 1.5 %collective-permute-done.2 = bf16[256,1032]{0,1:T(8,128)(2,1)S(1)} collective-permute-done((bf16[256,1032]{0,1:T(8,128)(2,1)S(1)}, bf16[256,1032]{0,1:T(8,128)(2,1)S(1)}, u32[]{:S(2)}, u32[]{:S(2)}) %collective-permute-start.2) | collective-permute-done | bytes 528416 | tf_op jit(solution)/shard_map/ppermute | solution.py:330
  113.4 0.4 shard_map.112
  113.8 5.0 %shard_map.114 = bf16[256,2048]{1,0:T(8,128)(2,1)} custom-call(bf16[256,2048]{1,0:T(8,128)(2,1)S(1)} %get-tuple-element.13.features_ref, f32[256,128]{1,0:T(8,128)S(1)} %get-tuple-element.14.scale_ref, bf16[2048,2048]{1,0:T(8,128)(2,1)} %all-gather.2.cloned.1.call-done.weight_ref), custom_call_target="tpu_custom_call" | custom-call | flops 2147483648 | bytes 8388608 | tf_op jit(solution)/shard_map/pallas_call | solution.py:312
  (33 shorter events, 0.1 us)
Async XLA Ops:
  6.5 33.1 %copy-start.1 = (bf16[1,256,256]{2,1,0:T(8,128)(2,1)S(1)}, bf16[1,256,256]{2,1,0:T(8,128)(2,1)}, u32[]{:S(2)}) copy-start(bf16[1,256,256]{2,1,0:T(8,128)(2,1)} %param.12) | copy-start | bytes 393220
  6.5 33.1 %copy-start = (bf16[1,256,1024]{2,1,0:T(8,128)(2,1)S(1)}, bf16[1,256,1024]{2,1,0:T(8,128)(2,1)}, u32[]{:S(2)}) copy-start(bf16[1,256,1024]{2,1,0:T(8,128)(2,1)} %param.11) | copy-start | bytes 1572868
  6.5 107.3 %all-gather.2.cloned.1.call-start = ((), (), s32[]{:S(2)}) async-start(), calls=%async_computation.3 | async-start | bytes 9437184 | tf_op jit(solution)/shard_map/all_gather | solution.py:220
  6.5 1.0 copy-start.2
  7.5 31.1 %copy-start.9 = (f32[1,16]{1,0:T(1,128)S(1)}, f32[1,16]{1,0:T(1,128)}, u32[]{:S(2)}) copy-start(f32[1,16]{1,0:T(1,128)} %param.16) | copy-start | bytes 196
  7.5 31.1 %copy-start.6 = (f32[1,16,256]{2,1,0:T(8,128)S(1)}, f32[1,16,256]{2,1,0:T(8,128)}, u32[]{:S(2)}) copy-start(f32[1,16,256]{2,1,0:T(8,128)} %param.14) | copy-start | bytes 49156
  7.5 31.1 %copy-start.8 = (f32[1,16]{1,0:T(1,128)S(1)}, f32[1,16]{1,0:T(1,128)}, u32[]{:S(2)}) copy-start(f32[1,16]{1,0:T(1,128)} %param.15) | copy-start | bytes 196
  7.5 32.1 %copy-start.3 = (f32[1,4,1024]{2,1,0:T(4,128)S(1)}, f32[1,4,1024]{2,1,0:T(4,128)}, u32[]{:S(2)}) copy-start(f32[1,4,1024]{2,1,0:T(4,128)} %param.18) | copy-start | bytes 49156
  7.5 32.1 %copy-start.4 = (f32[1,4,256]{2,1,0:T(4,128)S(1)}, f32[1,4,256]{2,1,0:T(4,128)}, u32[]{:S(2)}) copy-start(f32[1,4,256]{2,1,0:T(4,128)} %param.19) | copy-start | bytes 12292
  7.5 66.5 %copy-start.5 = (bf16[1,256,1024]{2,1,0:T(8,128)(2,1)S(1)}, bf16[1,256,1024]{2,1,0:T(8,128)(2,1)}, u32[]{:S(2)}) copy-start(bf16[1,256,1024]{2,1,0:T(8,128)(2,1)} %param.13) | copy-start | bytes 1572868
  33.1 54.9 %copy-start.10 = (f32[1,16]{1,0:T(1,128)S(1)}, f32[1,16]{1,0:T(1,128)}, u32[]{:S(2)}) copy-start(f32[1,16]{1,0:T(1,128)} %param.17) | copy-start | bytes 196
  34.4 5.1 %collective-permute-start = (bf16[8,1280]{1,0:T(8,128)(2,1)}, bf16[8,1280]{1,0:T(8,128)(2,1)S(1)}, u32[]{:S(2)}, u32[]{:S(2)}) collective-permute-start(bf16[8,1280]{1,0:T(8,128)(2,1)} %shard_map.109), channel_id=1, source_target_pairs={{0,2},{2,4},{4,6},{6,8},{8,10},{10,12},{12,14},{14,16},{16,18},{18... | collective-permute-start | bytes 61448 | tf_op jit(solution)/shard_map/ppermute | solution.py:32
  68.6 19.0 %all-to-all-start.1 = ((bf16[64,16,128]{2,1,0:T(8,128)(2,1)}), bf16[64,16,128]{2,1,0:T(8,128)(2,1)S(1)}, u32[]{:S(2)}, u32[]{:S(2)}) async-start(bf16[64,16,128]{2,1,0:T(8,128)(2,1)} %shard_map.111), calls=%async_computation.1 | async-start | bytes 524288 | tf_op jit(solution)/shard_map/all_to_all | solution.py:66
  87.9 1.7 %copy-start.7 = (f32[1,1024]{1,0:T(1,128)S(1)}, f32[1,1024]{1,0:T(1,128)}, u32[]{:S(2)}) copy-start(f32[1,1024]{1,0:T(1,128)} %param.20) | copy-start | bytes 12292
  90.2 11.6 %collective-permute-start.1 = (bf16[256,1032]{0,1:T(8,128)(2,1)S(1)}, bf16[256,1032]{0,1:T(8,128)(2,1)S(1)}, u32[]{:S(2)}, u32[]{:S(2)}) collective-permute-start(bf16[256,1032]{0,1:T(8,128)(2,1)S(1)} %concatenate.11), channel_id=1, source_target_pairs={{0,128},{128,256},{256,384},{384,0},{1,129},{129,257},{257,385},{3... | collective-permute-start | bytes 1585160 | tf_op jit(solution)/shard_map/ppermute | solution.py:336
  101.8 11.6 %collective-permute-start.2 = (bf16[256,1032]{0,1:T(8,128)(2,1)S(1)}, bf16[256,1032]{0,1:T(8,128)(2,1)S(1)}, u32[]{:S(2)}, u32[]{:S(2)}) collective-permute-start(bf16[256,1032]{0,1:T(8,128)(2,1)S(1)} %collective-permute-done.1), channel_id=1, source_target_pairs={{0,1},{1,0},{2,3},{3,2},{4,5},{5,4},{6,7},{7,6},{8,9},{9,8},{10,11... | collective-permute-start | bytes 1585160 | tf_op jit(solution)/shard_map/ppermute | solution.py:330
Sparse Core Ops, SparseCore 0:
  33.2 73.1 all-gather.1

commit v4 on v3

--- a/solution.py
+++ b/solution.py
@@ -14,6 +14,7 @@
 CTX_SIDE = 8
 EXTRA = 8
 TAIL = 8
+WHOLE_VMEM = 67043328
 
 
 NORM_FLOOR = 0.25
@@ -49,11 +50,11 @@
         )
 
 
-def states_before(sent, axes):
+def scanned_slices(sent, axes):
     count, rows, width = sent.shape
     rows = rows - EXTRA
     pieces = lax.all_to_all(sent, axes, 0, 0, tiled=True)
-    prior = pl.pallas_call(
+    return pl.pallas_call(
         scan_kernel,
         out_shape=jax.ShapeDtypeStruct((count, rows, width), jnp.bfloat16),
         in_specs=[pl.BlockSpec(memory_space=pltpu.VMEM)],
@@ -63,8 +64,6 @@
             flops=3 * count * rows * width, bytes_accessed=4 * count * rows * width, transcendentals=0
         ),
     )(pieces)
-    back = lax.all_to_all(prior, axes, 0, 0, tiled=True)
-    return back.reshape(count * rows, width)
 
 
 ALL_AXES = ("section", *CTX, "mp")
@@ -99,25 +98,50 @@
             pl.BlockSpec((TAIL, narrow.shape[1]), lambda i: (last, 0)),
         ],
         out_specs=pl.BlockSpec((TAIL, width), lambda i: (0, 0)),
+        compiler_params=pltpu.CompilerParams(vmem_limit_bytes=WHOLE_VMEM),
         cost_estimate=pl.CostEstimate(flops=0, bytes_accessed=4 * TAIL * width, transcendentals=0),
     )(wide, narrow)
 
 
-def copies_kernel(rows_ref, copies_ref):
-    rows = rows_ref[...]
-    for k in range(copies_ref.shape[0]):
-        copies_ref[k] = rows
-
-
-def copied(rows):
+def copies_kernel(rows_ref, copies_ref, held_ref, loaded, stored):
+    count, rows, _ = copies_ref.shape
+    chunks = loaded.shape[0]
+    size = rows // chunks
+
+    def load(chunk):
+        part = pl.ds(chunk * size, size)
+        return pltpu.make_async_copy(rows_ref.at[part], held_ref.at[part], loaded.at[chunk])
+
+    def store(chunk, k):
+        part = pl.ds(chunk * size, size)
+        return pltpu.make_async_copy(
+            held_ref.at[part], copies_ref.at[k, part], stored.at[chunk, k]
+        )
+
+    for chunk in range(chunks):
+        load(chunk).start()
+    for chunk in range(chunks):
+        load(chunk).wait()
+        for k in range(count):
+            store(chunk, k).start()
+    for chunk in range(chunks):
+        for k in range(count):
+            store(chunk, k).wait()
+
+
+def copied(rows, chunks=2):
     count = lax.axis_size(CTX[0])
-    vmem = pl.BlockSpec(memory_space=pltpu.VMEM)
+    anywhere = pl.BlockSpec(memory_space=pl.ANY)
     return pl.pallas_call(
         copies_kernel,
         out_shape=jax.ShapeDtypeStruct((count, *rows.shape), rows.dtype),
-        in_specs=[vmem],
-        out_specs=vmem,
-        compiler_params=small_vmem(4),
+        in_specs=[anywhere],
+        out_specs=anywhere,
+        scratch_shapes=[
+            pltpu.VMEM(rows.shape, rows.dtype),
+            pltpu.SemaphoreType.DMA((chunks,)),
+            pltpu.SemaphoreType.DMA((chunks, count)),
+        ],
         cost_estimate=pl.CostEstimate(
             flops=0, bytes_accessed=2 * (count + 1) * rows.size, transcendentals=0
         ),
@@ -129,6 +153,34 @@
         copies, ALL_AXES, 0, 0, axis_index_groups=crossed_groups(True), tiled=True
     )
     return pieces.reshape(-1, copies.shape[2])
+
+
+def load_kernel(*refs):
+    count = len(refs) // 2
+    sems = refs[-1]
+    copies = [
+        pltpu.make_async_copy(refs[k], refs[count + k], sems.at[k]) for k in range(count)
+    ]
+    for copy in copies:
+        copy.start()
+    for copy in copies:
+        copy.wait()
+
+
+def loaded(*arrays):
+    vmem = pl.BlockSpec(memory_space=pltpu.VMEM)
+    anywhere = pl.BlockSpec(memory_space=pl.ANY)
+    return pl.pallas_call(
+        load_kernel,
+        out_shape=[jax.ShapeDtypeStruct(x.shape, x.dtype) for x in arrays],
+        in_specs=[anywhere] * len(arrays),
+        out_specs=[vmem] * len(arrays),
+        scratch_shapes=[pltpu.SemaphoreType.DMA((len(arrays),))],
+        compiler_params=small_vmem(4),
+        cost_estimate=pl.CostEstimate(
+            flops=0, bytes_accessed=4 * sum(x.size for x in arrays), transcendentals=0
+        ),
+    )(*arrays)
 
 
 def prepare_kernel(
@@ -276,22 +328,29 @@
     )(core, own, other)
 
 
-def project_kernel(features_ref, scale_ref, weight_ref, out_ref, rows_ref, total_ref, arrived):
+def project_kernel(
+    features_ref, scale_ref, weight_ref, out_ref, rows_ref, total_ref, arrived, held_ref, left
+):
     depth, width = rows_ref.shape
     steps = arrived.shape[0]
+    parts = left.shape[0]
     block = depth // steps
-    part_width = 512
+    part_width = width // parts
 
     def fetch(step):
         rows = pl.ds(step * block, block)
         return pltpu.make_async_copy(weight_ref.at[rows], rows_ref.at[rows], arrived.at[step])
+
+    def store(part):
+        columns = pl.ds(part * part_width, part_width)
+        return pltpu.make_async_copy(held_ref.at[:, columns], out_ref.at[:, columns], left.at[part])
 
     for step in range(steps):
         fetch(step).start()
     for step in range(steps):
         fetch(step).wait()
-        for start in range(0, width, part_width):
-            columns = slice(start, start + part_width)
+        for part in range(parts):
+            columns = slice(part * part_width, (part + 1) * part_width)
             product = jnp.dot(
                 features_ref[:, step * block : (step + 1) * block],
                 rows_ref[step * block : (step + 1) * block, columns],
@@ -302,22 +361,28 @@
             if step < steps - 1:
                 total_ref[:, columns] = product
             else:
-                out_ref[:, columns] = (product * scale_ref[:, 0:1]).astype(out_ref.dtype)
-
-
-def projected(features, scale, weight, steps=8):
+                held_ref[:, columns] = (product * scale_ref[:, 0:1]).astype(held_ref.dtype)
+                store(part).start()
+    for part in range(parts):
+        store(part).wait()
+
+
+def projected(features, scale, weight, steps=8, parts=4):
     tokens, depth = features.shape
     width = weight.shape[1]
     vmem = pl.BlockSpec(memory_space=pltpu.VMEM)
+    anywhere = pl.BlockSpec(memory_space=pl.ANY)
     return pl.pallas_call(
         project_kernel,
         out_shape=jax.ShapeDtypeStruct((tokens, width), jnp.bfloat16),
-        in_specs=[vmem, vmem, pl.BlockSpec(memory_space=pl.ANY)],
-        out_specs=vmem,
+        in_specs=[vmem, vmem, anywhere],
+        out_specs=anywhere,
         scratch_shapes=[
             pltpu.VMEM((depth, width), weight.dtype),
             pltpu.VMEM((tokens, width), jnp.float32),
             pltpu.SemaphoreType.DMA((steps,)),
+            pltpu.VMEM((tokens, width), jnp.bfloat16),
+            pltpu.SemaphoreType.DMA((parts,)),
         ],
         compiler_params=small_vmem(52),
         cost_estimate=pl.CostEstimate(
@@ -334,6 +399,12 @@
     count = lax.axis_size(axis)
     pairs = [(source, (source + steps) % count) for source in range(count)]
     return lax.ppermute(value, axis, pairs)
+
+
+def causal(offset):
+    row_index = lax.broadcasted_iota(jnp.int32, (BLOCK, BLOCK), 0)
+    col_index = lax.broadcasted_iota(jnp.int32, (BLOCK, BLOCK), 1)
+    return row_index >= col_index + offset
 
 
 def section_block(
@@ -361,22 +432,32 @@
     log_decay = -jnp.exp(decay_log[0])[:, None] * step_size
     blocks_step = step_size.reshape(head_count, block_count, BLOCK)
     blocks_decay = log_decay.reshape(head_count, block_count, BLOCK)
-    row_index = lax.broadcasted_iota(jnp.int32, (BLOCK, BLOCK), 0)
-    col_index = lax.broadcasted_iota(jnp.int32, (BLOCK, BLOCK), 1)
-    causal_mask = row_index >= col_index
-    lower_tri = causal_mask.astype(jnp.float32)
+    offset = jnp.zeros((), jnp.int32)
+    lower_tri = causal(offset).astype(jnp.float32)
     cumulative = jnp.einsum("hcs,ts->hct", blocks_decay, lower_tri, precision=HIGHEST)
     tail_weight = jnp.exp(cumulative[..., -1:] - cumulative) * blocks_step
+    wide, narrow, wide_taps, narrow_taps = loaded(
+        head_input[0], state_proj[0], conv_head[0], conv_state[0]
+    )
     conv_xt, conv_bc, sent = prepared(
-        head_input[0],
-        state_proj[0],
+        wide,
+        narrow,
         behind,
-        conv_head[0],
-        conv_state[0],
+        wide_taps,
+        narrow_taps,
         tail_weight[:, 0],
         cumulative[:, 0, -1],
         CTX,
     )
+    full_weight = gathered_weight(part)
+    prior = scanned_slices(sent, CTX)
+    prior, conv_xt, conv_bc, gate_input, offset = lax.optimization_barrier(
+        (prior, conv_xt, conv_bc, gate_input, offset)
+    )
+    prior_state = lax.all_to_all(prior, CTX, 0, 0, tiled=True).reshape(
+        head_count, head_width, STATE
+    )
+    causal_mask = causal(offset)
     blocks_x = conv_xt.T.reshape(block_count, BLOCK, head_count, head_width)
     blocks_b = conv_bc[:, :STATE].reshape(block_count, BLOCK, STATE)
     blocks_c = conv_bc[:, STATE:].reshape(block_count, BLOCK, STATE)
@@ -388,18 +469,14 @@
     intra_part = jnp.einsum(
         "hcts,cshp->cthp", mix_weight, blocks_x, preferred_element_type=jnp.float32
     )
-    full_weight = gathered_weight(part)
-    prior_state = states_before(sent, CTX).reshape(head_count, head_width, STATE)
+    local_part = intra_part + skip_gain[0][None, None, :, None] * blocks_x.astype(jnp.float32)
+    gate = jax.nn.silu(gate_input[0].astype(jnp.float32))
+    local_part, gate = lax.optimization_barrier((local_part, gate))
     inter_part = (
         jnp.einsum("ctn,hpn->cthp", blocks_c, prior_state, preferred_element_type=jnp.float32)
         * jnp.exp(cumulative).transpose(1, 2, 0)[..., None]
     )
-    output = (
-        intra_part + inter_part + skip_gain[0][None, None, :, None] * blocks_x.astype(jnp.float32)
-    )
-    gated = output.reshape(token_count, local_width) * jax.nn.silu(
-        gate_input[0].astype(jnp.float32)
-    )
+    gated = (local_part + inter_part).reshape(token_count, local_width) * gate
     high, low = split_in_two(jnp.sum(gated * gated, axis=1))
     extra = jnp.stack([high, low] + [jnp.zeros_like(high)] * (EXTRA - 2), axis=1)
     features = (gated * norm_gain[0][None]).astype(jnp.bfloat16)

time: 126 us -> 129 us (1.024)
  local copies, waits for them, and re-layouts: 2.09 us -> 5.49 us
  waiting for transfers between devices: 23.2 us -> 20.5 us
  other arithmetic: 0.69 us -> 2.99 us
  Pallas kernels: 8.72 us -> 10.7 us
  blocking collectives: 52.5 us -> 51 us
    all_to_all x1, waiting for transfers between devices: 13.2 us -> 10.5 us  [section_block(): lax.all_to_all(prior, CTX, 0, 0, tiled=True)]
    ppermute x1, starting transfers between devices: 10 us -> 7.85 us  [other_half(): return lax.ppermute(x, axis, [(0, 1), (1, 0)])]
    unnamed x23 -> x12, local copies, waits for them, and re-layouts: 1.21 us -> 3.36 us
    pallas_call x1, Pallas kernels: 0.07 us -> 1.94 us  [copied(): pl.pallas_call(copies_kernel, out_shape=jax.ShapeDtypeStruct((count, *row...]
    all_to_all x1, starting transfers between devices: 5.41 us -> 6.95 us  [section_block(): lax.all_to_all(prior, CTX, 0, 0, tiled=True)]
    all_to_all x1, blocking collectives: 27 us -> 25.5 us  [scanned_slices(): pieces = lax.all_to_all(sent, axes, 0, 0, tiled=True)]
  transfers between devices with their start and end apart: 5 -> 5, of which waited for: 3 -> 3; matrix products, arithmetic and copies ran while one was open for 3% -> 6% of each run, Pallas kernels for 3% -> 3%
where the time goes in v4:
time: 129 us; the launch traced here: 128 us
  blocking collectives  51 us (40%)
  starting transfers between devices  22 us (17%)
  waiting for transfers between devices  20.5 us (16%)
  between operations  13.6 us (11%)
  Pallas kernels  10.7 us (8%)
  local copies, waits for them, and re-layouts  5.49 us (4%)
  other arithmetic  2.99 us (2%)
  matrix products  2.02 us (2%)
    all_to_all x1, blocking collectives, scanned_slices(): pieces = lax.all_to_all(sent, axes, 0, 0, tiled=True)  25.5 us
    all_to_all x1, blocking collectives, weight_part(): lax.all_to_all(copies, ALL_AXES, 0, 0, axis_index_groups=crossed_groups(T...  25.5 us
    all_to_all x1, waiting for transfers between devices, section_block(): lax.all_to_all(prior, CTX, 0, 0, tiled=True)  10.5 us
    ppermute x1, waiting for transfers between devices, shifted(): return lax.ppermute(value, axis, pairs)  8.45 us
    ppermute x1, starting transfers between devices, other_half(): return lax.ppermute(x, axis, [(0, 1), (1, 0)])  7.85 us
    all_to_all x1, starting transfers between devices, section_block(): lax.all_to_all(prior, CTX, 0, 0, tiled=True)  6.95 us
    pallas_call x1, Pallas kernels, projected(): pl.pallas_call(project_kernel, out_shape=jax.ShapeDtypeStruct((tokens, wi...  4.82 us
    ppermute x1, starting transfers between devices, from_behind(): lax.ppermute(value, axis, [(source, source + steps) for source in range(f...  4.12 us
  transfers between devices with their start and end apart: 5, of which 3 were waited for; matrix products, arithmetic and copies ran while one was open for 6% of the time, Pallas kernels for 3%

profile of v4, /device:TPU:1, one launch (start us, length us, event | category | flops | bytes accessed | tf_op | source)
XLA Modules:
  0.0 128.4 jit_solution(5798599878159273225)
XLA Ops:
  6.5 1.9 %shard_map.114 = bf16[8,32,2048]{2,1,0:T(8,128)(2,1)} custom-call(bf16[32,2048]{1,0:T(8,128)(2,1)} %bitcast.75), custom_call_target="tpu_custom_call" | custom-call | bytes 1179648 | tf_op jit(solution)/shard_map/pallas_call | solution.py:135
  8.5 25.5 %all_to_all.15 = bf16[8,32,2048]{2,1,0:T(8,128)(2,1)} all-to-all(bf16[8,32,2048]{2,1,0:T(8,128)(2,1)} %shard_map.114), channel_id=1, replica_groups={{0,2,4,6,8,10,12,14},{16,18,20,22,24,26,28,30},{32,34,36,38,40,42,44,46..., dimensions={0} | all-to-all | bytes 2097152 | tf_op jit(solution)/shard_map/all_to_all | solution.py:152
  34.0 1.3 %shard_map.110 = bf16[8,1280]{1,0:T(8,128)(2,1)} custom-call(bf16[256,1024]{1,0:T(8,128)(2,1)} %bitcast.63, bf16[256,256]{1,0:T(8,128)(2,1)} %bitcast.67), custom_call_target="tpu_custom_call" | custom-call | bytes 40960 | tf_op jit(solution)/shard_map/pallas_call | solution.py:92
  35.4 4.1 %collective-permute-start = (bf16[8,1280]{1,0:T(8,128)(2,1)}, bf16[8,1280]{1,0:T(8,128)(2,1)S(1)}, u32[]{:S(2)}, u32[]{:S(2)}) collective-permute-start(bf16[8,1280]{1,0:T(8,128)(2,1)} %shard_map.110), channel_id=1, source_target_pairs={{0,2},{2,4},{4,6},{6,8},{8,10},{10,12},{12,14},{14,16},{16,18},{18... | collective-permute-start | bytes 61448 | tf_op jit(solution)/shard_map/ppermute | solution.py:33
  39.7 0.7 negate_bitcast_fusion
  40.3 0.8 compare_select_fusion
  41.1 0.2 fusion.14
  41.3 0.3 exponential_reduce_fusion
  41.8 0.8 exponential_bitcast_fusion
  42.7 1.0 copy-done
  43.7 0.9 copy-done.1
  44.7 0.7 copy-done.2
  45.4 0.7 copy-done.3
  46.1 0.3 shard_map.109
  46.4 1.1 shard_map.111
  47.5 25.5 %all_to_all.16.pieces_ref = bf16[64,24,128]{2,1,0:T(8,128)(2,1)S(1)} all-to-all(bf16[64,24,128]{2,1,0:T(8,128)(2,1)S(1)} %get-tuple-element.25), channel_id=1, replica_groups=mesh['section'=4,'ctx_0'=8,'ctx_1'=8,'mp'=2] {'ctx_0','ctx_1'}, dimensions={0} | all-to-all | bytes 786432 | tf_op jit(solution)/shard_map/all_to_all | solution.py:56
  73.0 0.8 shard_map.112
  73.9 6.9 %all-to-all-start.1 = ((bf16[64,16,128]{2,1,0:T(8,128)(2,1)}), bf16[64,16,128]{2,1,0:T(8,128)(2,1)S(1)}, u32[]{:S(2)}, u32[]{:S(2)}) async-start(bf16[64,16,128]{2,1,0:T(8,128)(2,1)} %shard_map.112), calls=%async_computation.1 | async-start | bytes 524288 | tf_op jit(solution)/shard_map/all_to_all | solution.py:457
  80.8 1.3 copy.17
  82.1 0.2 fusion.16
  82.3 0.3 convert_multiply_fusion
  82.6 1.4 %fusion.9 = f32[1,256,16,64]{1,3,2,0:T(8,128)S(1)} fusion(bf16[256,16,64]{0,2,1:T(8,128)(2,1)S(1)} %bitcast.71, f32[16,256]{1,0:T(8,128)S(1)} %compare_select_fusion, f32[16,256]{1,0:T(8,128)S(1)} %fusion.14, f32[256,256]{1,0:T(8,128)S(1)} %fusion.16, pred[256,256]{1,0:T(8,128)(4,1)S(1)} %iota_compare_fusion, bf16[1,256,16,64]{1,3,2,0:T(8,128)(2,1)S(1)} %bitcast.72, ...), kind=kOutput, calls=%fused_computation.11 | convolution fusion | flops 141295616 | bytes 2457664 | tf_op jit(solution)/shard_map/hcts,cshp->cthp/dot_general | solution.py:469
  84.0 10.5 %all-to-all-done.1 = bf16[64,16,128]{2,1,0:T(8,128)(2,1)S(1)} async-done(((bf16[64,16,128]{2,1,0:T(8,128)(2,1)}), bf16[64,16,128]{2,1,0:T(8,128)(2,1)S(1)}, u32[]{:S(2)}, u32[]{:S(2)}) %all-to-all-start.1) | async-done | bytes 262176 | tf_op jit(solution)/shard_map/all_to_all | solution.py:457
  94.5 0.3 fusion.10
  94.8 0.3 multiply_reduce_fusion
  95.1 0.2 concatenate.11
  95.2 3.1 %collective-permute-start.1 = (bf16[256,1032]{0,1:T(8,128)(2,1)S(1)}, bf16[256,1032]{0,1:T(8,128)(2,1)S(1)}, u32[]{:S(2)}, u32[]{:S(2)}) collective-permute-start(bf16[256,1032]{0,1:T(8,128)(2,1)S(1)} %concatenate.11), channel_id=1, source_target_pairs={{0,128},{128,256},{256,384},{384,0},{1,129},{129,257},{257,385},{3... | collective-permute-start | bytes 1585160 | tf_op jit(solution)/shard_map/ppermute | solution.py:401
  98.4 8.5 %collective-permute-done.1 = bf16[256,1032]{0,1:T(8,128)(2,1)S(1)} collective-permute-done((bf16[256,1032]{0,1:T(8,128)(2,1)S(1)}, bf16[256,1032]{0,1:T(8,128)(2,1)S(1)}, u32[]{:S(2)}, u32[]{:S(2)}) %collective-permute-start.1) | collective-permute-done | bytes 528416 | tf_op jit(solution)/shard_map/ppermute | solution.py:401
  106.8 7.8 %collective-permute-start.2 = (bf16[256,1032]{0,1:T(8,128)(2,1)S(1)}, bf16[256,1032]{0,1:T(8,128)(2,1)S(1)}, u32[]{:S(2)}, u32[]{:S(2)}) collective-permute-start(bf16[256,1032]{0,1:T(8,128)(2,1)S(1)} %collective-permute-done.1), channel_id=1, source_target_pairs={{0,1},{1,0},{2,3},{3,2},{4,5},{5,4},{6,7},{7,6},{8,9},{9,8},{10,11... | collective-permute-start | bytes 1585160 | tf_op jit(solution)/shard_map/ppermute | solution.py:395
  114.7 1.5 %collective-permute-done.2 = bf16[256,1032]{0,1:T(8,128)(2,1)S(1)} collective-permute-done((bf16[256,1032]{0,1:T(8,128)(2,1)S(1)}, bf16[256,1032]{0,1:T(8,128)(2,1)S(1)}, u32[]{:S(2)}, u32[]{:S(2)}) %collective-permute-start.2) | collective-permute-done | bytes 528416 | tf_op jit(solution)/shard_map/ppermute | solution.py:395
  116.2 0.4 shard_map.113
  116.7 4.8 %shard_map.115 = bf16[256,2048]{1,0:T(8,128)(2,1)} custom-call(bf16[256,2048]{1,0:T(8,128)(2,1)S(1)} %get-tuple-element.35.features_ref, f32[256,128]{1,0:T(8,128)S(1)} %get-tuple-element.36.scale_ref, bf16[2048,2048]{1,0:T(8,128)(2,1)} %all-gather.2.cloned.1.call-done.weight_ref), custom_call_target="tpu_custom_call" | custom-call | flops 2147483648 | bytes 8388608 | tf_op jit(solution)/shard_map/pallas_call | solution.py:375
  (26 shorter events, 0.6 us)
Async XLA Ops:
  6.5 110.1 %all-gather.2.cloned.1.call-start = ((), (), s32[]{:S(2)}) async-start(), calls=%async_computation.3 | async-start | bytes 9437184 | tf_op jit(solution)/shard_map/all_gather | solution.py:272
  35.4 47.3 %copy-start.5 = (f32[1,16]{1,0:T(1,128)S(1)}, f32[1,16]{1,0:T(1,128)}, u32[]{:S(2)}) copy-start(f32[1,16]{1,0:T(1,128)} %param.17) | copy-start | bytes 196
  35.4 11.0 %collective-permute-start = (bf16[8,1280]{1,0:T(8,128)(2,1)}, bf16[8,1280]{1,0:T(8,128)(2,1)S(1)}, u32[]{:S(2)}, u32[]{:S(2)}) collective-permute-start(bf16[8,1280]{1,0:T(8,128)(2,1)} %shard_map.110), channel_id=1, source_target_pairs={{0,2},{2,4},{4,6},{6,8},{8,10},{10,12},{12,14},{14,16},{16,18},{18... | collective-permute-start | bytes 61448 | tf_op jit(solution)/shard_map/ppermute | solution.py:33
  42.7 1.0 copy-start
  43.7 0.9 copy-start.1
  44.6 0.7 copy-start.2
  45.4 0.7 copy-start.3
  73.9 20.6 %all-to-all-start.1 = ((bf16[64,16,128]{2,1,0:T(8,128)(2,1)}), bf16[64,16,128]{2,1,0:T(8,128)(2,1)S(1)}, u32[]{:S(2)}, u32[]{:S(2)}) async-start(bf16[64,16,128]{2,1,0:T(8,128)(2,1)} %shard_map.112), calls=%async_computation.1 | async-start | bytes 524288 | tf_op jit(solution)/shard_map/all_to_all | solution.py:457
  82.6 12.1 %copy-start.4 = (f32[1,1024]{1,0:T(1,128)S(1)}, f32[1,1024]{1,0:T(1,128)}, u32[]{:S(2)}) copy-start(f32[1,1024]{1,0:T(1,128)} %param.20) | copy-start | bytes 12292
  95.2 11.6 %collective-permute-start.1 = (bf16[256,1032]{0,1:T(8,128)(2,1)S(1)}, bf16[256,1032]{0,1:T(8,128)(2,1)S(1)}, u32[]{:S(2)}, u32[]{:S(2)}) collective-permute-start(bf16[256,1032]{0,1:T(8,128)(2,1)S(1)} %concatenate.11), channel_id=1, source_target_pairs={{0,128},{128,256},{256,384},{384,0},{1,129},{129,257},{257,385},{3... | collective-permute-start | bytes 1585160 | tf_op jit(solution)/shard_map/ppermute | solution.py:401
  106.8 9.4 %collective-permute-start.2 = (bf16[256,1032]{0,1:T(8,128)(2,1)S(1)}, bf16[256,1032]{0,1:T(8,128)(2,1)S(1)}, u32[]{:S(2)}, u32[]{:S(2)}) collective-permute-start(bf16[256,1032]{0,1:T(8,128)(2,1)S(1)} %collective-permute-done.1), channel_id=1, source_target_pairs={{0,1},{1,0},{2,3},{3,2},{4,5},{5,4},{6,7},{7,6},{8,9},{9,8},{10,11... | collective-permute-start | bytes 1585160 | tf_op jit(solution)/shard_map/ppermute | solution.py:395
Sparse Core Ops, SparseCore 0:
  34.1 73.1 all-gather.1

commit v5 on v4

--- a/solution.py
+++ b/solution.py
@@ -13,6 +13,7 @@
 CTX = ("ctx_0", "ctx_1")
 CTX_SIDE = 8
 EXTRA = 8
+PAIR = 2
 TAIL = 8
 WHOLE_VMEM = 67043328
 
@@ -39,20 +40,23 @@
 
 
 def scan_kernel(pieces_ref, prior_ref):
-    count, _, width = pieces_ref.shape
-    rows = prior_ref.shape[1]
-    carried = jnp.zeros((rows, width), jnp.float32)
+    count, pair, _ = pieces_ref.shape
+    _, rows, width = prior_ref.shape
+    parts = rows // pair
+    carried = [jnp.zeros((pair, width), jnp.float32) for _ in range(parts)]
     for k in range(count):
-        prior_ref[k] = carried.astype(jnp.bfloat16)
-        factor = pieces_ref[k, rows : rows + 2, :].astype(jnp.float32)
-        carried = (factor[0:1] + factor[1:2]) * carried + pieces_ref[k, 0:rows, :].astype(
-            jnp.float32
-        )
+        factor = pieces_ref[k, :, parts * width :].astype(jnp.float32)
+        factor = factor[0:1] + factor[1:2]
+        for part in range(parts):
+            prior_ref[k, part * pair : (part + 1) * pair, :] = carried[part].astype(jnp.bfloat16)
+            piece = pieces_ref[k, :, part * width : (part + 1) * width].astype(jnp.float32)
+            carried[part] = factor * carried[part] + piece
 
 
 def scanned_slices(sent, axes):
-    count, rows, width = sent.shape
-    rows = rows - EXTRA
+    count, pair, total = sent.shape
+    width = STATE
+    rows = pair * (total // width - 1)
     pieces = lax.all_to_all(sent, axes, 0, 0, tiled=True)
     return pl.pallas_call(
         scan_kernel,
@@ -196,6 +200,7 @@
     sent_ref,
     padded_ref,
     weighted_ref,
+    state_ref,
 ):
     tokens, width = wide_ref.shape
     heads = tail_weight_ref.shape[0]
@@ -232,11 +237,16 @@
     state = jnp.dot(
         weighted_ref[...], narrow_out_ref[:, :STATE], preferred_element_type=jnp.float32
     )
-    count, _, state_width = sent_ref.shape
-    rows = width // count
-    sent_ref[:, 0:rows, :] = state.astype(jnp.bfloat16).reshape(count, rows, state_width)
+    state_ref[...] = state
+    count, pair, total = sent_ref.shape
+    parts = total // STATE - 1
     for k in range(count):
-        sent_ref[k, rows:, :] = factors_ref[k * heads // count]
+        for part in range(parts):
+            start = (k * parts + part) * pair
+            sent_ref[k, :, part * STATE : (part + 1) * STATE] = state_ref[
+                start : start + pair, :
+            ].astype(jnp.bfloat16)
+        sent_ref[k, :, parts * STATE :] = factors_ref[k * heads // count, 0:pair, :]
 
 
 def prepared(wide, narrow, behind, wide_taps, narrow_taps, tail_weight, total_log, axes):
@@ -245,19 +255,21 @@
     high, low = split_in_two(jnp.exp(total_log))
     factors = jnp.stack([high, low] + [jnp.zeros_like(high)] * (EXTRA - 2), axis=1)
     factors = jnp.broadcast_to(factors[:, :, None], (*factors.shape, STATE))
+    slice_width = (width // count // PAIR + 1) * STATE
     vmem = pl.BlockSpec(memory_space=pltpu.VMEM)
     return pl.pallas_call(
         prepare_kernel,
         out_shape=(
             jax.ShapeDtypeStruct((width, tokens), jnp.bfloat16),
             jax.ShapeDtypeStruct(narrow.shape, jnp.bfloat16),
-            jax.ShapeDtypeStruct((count, width // count + EXTRA, STATE), jnp.bfloat16),
+            jax.ShapeDtypeStruct((count, PAIR, slice_width), jnp.bfloat16),
         ),
         in_specs=[vmem] * 7,
         out_specs=(vmem, vmem, vmem),
         scratch_shapes=[
             pltpu.VMEM((TAIL + tokens, 128), jnp.float32),
             pltpu.VMEM((width, tokens), jnp.bfloat16),
+            pltpu.VMEM((width, STATE), jnp.float32),
         ],
         compiler_params=small_vmem(12),
     cost_estimate=pl.CostEstimate(

time: 129 us -> 127 us (0.984)
  blocking collectives: 51 us -> 49.7 us
    all_to_all x1, starting transfers between devices: 6.95 us -> 5.18 us  [section_block(): lax.all_to_all(prior, CTX, 0, 0, tiled=True)]
    all_to_all x1, blocking collectives: 25.5 us -> 24.2 us  [scanned_slices(): pieces = lax.all_to_all(sent, axes, 0, 0, tiled=True)]
where the time goes in v5:
time: 127 us; the launch traced here: 126 us
  blocking collectives  49.7 us (39%)
  starting transfers between devices  21 us (17%)
  waiting for transfers between devices  20.4 us (16%)
  between operations  13.6 us (11%)
  Pallas kernels  11 us (9%)
  local copies, waits for them, and re-layouts  5.48 us (4%)
  other arithmetic  2.99 us (2%)
  matrix products  2.03 us (2%)
    all_to_all x1, blocking collectives, weight_part(): lax.all_to_all(copies, ALL_AXES, 0, 0, axis_index_groups=crossed_groups(T...  25.5 us
    all_to_all x1, blocking collectives, scanned_slices(): pieces = lax.all_to_all(sent, axes, 0, 0, tiled=True)  24.2 us
    all_to_all x1, waiting for transfers between devices, section_block(): lax.all_to_all(prior, CTX, 0, 0, tiled=True)  10.4 us
    ppermute x1, starting transfers between devices, other_half(): return lax.ppermute(x, axis, [(0, 1), (1, 0)])  8.5 us
    ppermute x1, waiting for transfers between devices, shifted(): return lax.ppermute(value, axis, pairs)  8.41 us
    all_to_all x1, starting transfers between devices, section_block(): lax.all_to_all(prior, CTX, 0, 0, tiled=True)  5.18 us
    pallas_call x1, Pallas kernels, projected(): pl.pallas_call(project_kernel, out_shape=jax.ShapeDtypeStruct((tokens, wi...  4.81 us
    ppermute x1, starting transfers between devices, from_behind(): lax.ppermute(value, axis, [(source, source + steps) for source in range(f...  4.12 us
  transfers between devices with their start and end apart: 5, of which 3 were waited for; matrix products, arithmetic and copies ran while one was open for 6% of the time, Pallas kernels for 3%

profile of v5, /device:TPU:1, one launch (start us, length us, event | category | flops | bytes accessed | tf_op | source)
XLA Modules:
  0.0 126.2 jit_solution(6631813503910042269)
XLA Ops:
  6.5 1.9 %shard_map.114 = bf16[8,32,2048]{2,1,0:T(8,128)(2,1)} custom-call(bf16[32,2048]{1,0:T(8,128)(2,1)} %bitcast.75), custom_call_target="tpu_custom_call" | custom-call | bytes 1179648 | tf_op jit(solution)/shard_map/pallas_call | solution.py:139
  8.5 25.5 %all_to_all.15 = bf16[8,32,2048]{2,1,0:T(8,128)(2,1)} all-to-all(bf16[8,32,2048]{2,1,0:T(8,128)(2,1)} %shard_map.114), channel_id=1, replica_groups={{0,2,4,6,8,10,12,14},{16,18,20,22,24,26,28,30},{32,34,36,38,40,42,44,46..., dimensions={0} | all-to-all | bytes 2097152 | tf_op jit(solution)/shard_map/all_to_all | solution.py:156
  34.0 1.3 %shard_map.110 = bf16[8,1280]{1,0:T(8,128)(2,1)} custom-call(bf16[256,1024]{1,0:T(8,128)(2,1)} %bitcast.63, bf16[256,256]{1,0:T(8,128)(2,1)} %bitcast.67), custom_call_target="tpu_custom_call" | custom-call | bytes 40960 | tf_op jit(solution)/shard_map/pallas_call | solution.py:96
  35.4 4.1 %collective-permute-start = (bf16[8,1280]{1,0:T(8,128)(2,1)}, bf16[8,1280]{1,0:T(8,128)(2,1)S(1)}, u32[]{:S(2)}, u32[]{:S(2)}) collective-permute-start(bf16[8,1280]{1,0:T(8,128)(2,1)} %shard_map.110), channel_id=1, source_target_pairs={{0,2},{2,4},{4,6},{6,8},{8,10},{10,12},{12,14},{14,16},{16,18},{18... | collective-permute-start | bytes 61448 | tf_op jit(solution)/shard_map/ppermute | solution.py:34
  39.7 0.7 negate_bitcast_fusion
  40.3 0.8 compare_select_fusion
  41.1 0.2 fusion.14
  41.3 0.3 exponential_reduce_fusion
  41.8 0.8 exponential_bitcast_fusion
  42.7 1.0 copy-done
  43.7 0.9 copy-done.1
  44.7 0.7 copy-done.2
  45.4 0.7 copy-done.3
  46.1 0.3 shard_map.109
  46.4 1.1 shard_map.111
  47.6 24.2 %all_to_all.16.pieces_ref = bf16[64,2,1152]{2,1,0:T(2,128)(2,1)S(1)} all-to-all(bf16[64,2,1152]{2,1,0:T(2,128)(2,1)S(1)} %get-tuple-element.25), channel_id=1, replica_groups=mesh['section'=4,'ctx_0'=8,'ctx_1'=8,'mp'=2] {'ctx_0','ctx_1'}, dimensions={0} | all-to-all | bytes 589824 | tf_op jit(solution)/shard_map/all_to_all | solution.py:60
  71.8 1.1 shard_map.112
  72.8 5.2 %all-to-all-start.1 = ((bf16[64,16,128]{2,1,0:T(8,128)(2,1)}), bf16[64,16,128]{2,1,0:T(8,128)(2,1)S(1)}, u32[]{:S(2)}, u32[]{:S(2)}) async-start(bf16[64,16,128]{2,1,0:T(8,128)(2,1)} %shard_map.112), calls=%async_computation.1 | async-start | bytes 524288 | tf_op jit(solution)/shard_map/all_to_all | solution.py:469
  78.0 1.3 copy.17
  79.3 0.2 fusion.16
  79.5 0.3 convert_multiply_fusion
  79.9 1.4 %fusion.9 = f32[1,256,16,64]{1,3,2,0:T(8,128)S(1)} fusion(bf16[256,16,64]{0,2,1:T(8,128)(2,1)S(1)} %bitcast.71, f32[16,256]{1,0:T(8,128)S(1)} %compare_select_fusion, f32[16,256]{1,0:T(8,128)S(1)} %fusion.14, f32[256,256]{1,0:T(8,128)S(1)} %fusion.16, pred[256,256]{1,0:T(8,128)(4,1)S(1)} %iota_compare_fusion, bf16[1,256,16,64]{1,3,2,0:T(8,128)(2,1)S(1)} %bitcast.72, ...), kind=kOutput, calls=%fused_computation.11 | convolution fusion | flops 141295616 | bytes 2457664 | tf_op jit(solution)/shard_map/hcts,cshp->cthp/dot_general | solution.py:481
  81.2 10.4 %all-to-all-done.1 = bf16[64,16,128]{2,1,0:T(8,128)(2,1)S(1)} async-done(((bf16[64,16,128]{2,1,0:T(8,128)(2,1)}), bf16[64,16,128]{2,1,0:T(8,128)(2,1)S(1)}, u32[]{:S(2)}, u32[]{:S(2)}) %all-to-all-start.1) | async-done | bytes 262176 | tf_op jit(solution)/shard_map/all_to_all | solution.py:469
  91.6 0.3 fusion.10
  92.0 0.3 multiply_reduce_fusion
  92.3 0.2 concatenate.11
  92.4 3.2 %collective-permute-start.1 = (bf16[256,1032]{0,1:T(8,128)(2,1)S(1)}, bf16[256,1032]{0,1:T(8,128)(2,1)S(1)}, u32[]{:S(2)}, u32[]{:S(2)}) collective-permute-start(bf16[256,1032]{0,1:T(8,128)(2,1)S(1)} %concatenate.11), channel_id=1, source_target_pairs={{0,128},{128,256},{256,384},{384,0},{1,129},{129,257},{257,385},{3... | collective-permute-start | bytes 1585160 | tf_op jit(solution)/shard_map/ppermute | solution.py:413
  95.6 8.4 %collective-permute-done.1 = bf16[256,1032]{0,1:T(8,128)(2,1)S(1)} collective-permute-done((bf16[256,1032]{0,1:T(8,128)(2,1)S(1)}, bf16[256,1032]{0,1:T(8,128)(2,1)S(1)}, u32[]{:S(2)}, u32[]{:S(2)}) %collective-permute-start.1) | collective-permute-done | bytes 528416 | tf_op jit(solution)/shard_map/ppermute | solution.py:413
  104.0 8.5 %collective-permute-start.2 = (bf16[256,1032]{0,1:T(8,128)(2,1)S(1)}, bf16[256,1032]{0,1:T(8,128)(2,1)S(1)}, u32[]{:S(2)}, u32[]{:S(2)}) collective-permute-start(bf16[256,1032]{0,1:T(8,128)(2,1)S(1)} %collective-permute-done.1), channel_id=1, source_target_pairs={{0,1},{1,0},{2,3},{3,2},{4,5},{5,4},{6,7},{7,6},{8,9},{9,8},{10,11... | collective-permute-start | bytes 1585160 | tf_op jit(solution)/shard_map/ppermute | solution.py:407
  112.5 1.5 %collective-permute-done.2 = bf16[256,1032]{0,1:T(8,128)(2,1)S(1)} collective-permute-done((bf16[256,1032]{0,1:T(8,128)(2,1)S(1)}, bf16[256,1032]{0,1:T(8,128)(2,1)S(1)}, u32[]{:S(2)}, u32[]{:S(2)}) %collective-permute-start.2) | collective-permute-done | bytes 528416 | tf_op jit(solution)/shard_map/ppermute | solution.py:407
  114.0 0.4 shard_map.113
  114.5 4.8 %shard_map.115 = bf16[256,2048]{1,0:T(8,128)(2,1)} custom-call(bf16[256,2048]{1,0:T(8,128)(2,1)S(1)} %get-tuple-element.35.features_ref, f32[256,128]{1,0:T(8,128)S(1)} %get-tuple-element.36.scale_ref, bf16[2048,2048]{1,0:T(8,128)(2,1)} %all-gather.2.cloned.1.call-done.weight_ref), custom_call_target="tpu_custom_call" | custom-call | flops 2147483648 | bytes 8388608 | tf_op jit(solution)/shard_map/pallas_call | solution.py:387
  (26 shorter events, 0.6 us)
Async XLA Ops:
  6.5 108.0 %all-gather.2.cloned.1.call-start = ((), (), s32[]{:S(2)}) async-start(), calls=%async_computation.3 | async-start | bytes 9437184 | tf_op jit(solution)/shard_map/all_gather | solution.py:284
  35.4 44.5 %copy-start.5 = (f32[1,16]{1,0:T(1,128)S(1)}, f32[1,16]{1,0:T(1,128)}, u32[]{:S(2)}) copy-start(f32[1,16]{1,0:T(1,128)} %param.17) | copy-start | bytes 196
  35.4 11.0 %collective-permute-start = (bf16[8,1280]{1,0:T(8,128)(2,1)}, bf16[8,1280]{1,0:T(8,128)(2,1)S(1)}, u32[]{:S(2)}, u32[]{:S(2)}) collective-permute-start(bf16[8,1280]{1,0:T(8,128)(2,1)} %shard_map.110), channel_id=1, source_target_pairs={{0,2},{2,4},{4,6},{6,8},{8,10},{10,12},{12,14},{14,16},{16,18},{18... | collective-permute-start | bytes 61448 | tf_op jit(solution)/shard_map/ppermute | solution.py:34
  42.7 1.0 copy-start
  43.7 0.9 copy-start.1
  44.6 0.7 copy-start.2
  45.4 0.7 copy-start.3
  72.8 18.8 %all-to-all-start.1 = ((bf16[64,16,128]{2,1,0:T(8,128)(2,1)}), bf16[64,16,128]{2,1,0:T(8,128)(2,1)S(1)}, u32[]{:S(2)}, u32[]{:S(2)}) async-start(bf16[64,16,128]{2,1,0:T(8,128)(2,1)} %shard_map.112), calls=%async_computation.1 | async-start | bytes 524288 | tf_op jit(solution)/shard_map/all_to_all | solution.py:469
  79.8 12.1 %copy-start.4 = (f32[1,1024]{1,0:T(1,128)S(1)}, f32[1,1024]{1,0:T(1,128)}, u32[]{:S(2)}) copy-start(f32[1,1024]{1,0:T(1,128)} %param.20) | copy-start | bytes 12292
  92.4 11.6 %collective-permute-start.1 = (bf16[256,1032]{0,1:T(8,128)(2,1)S(1)}, bf16[256,1032]{0,1:T(8,128)(2,1)S(1)}, u32[]{:S(2)}, u32[]{:S(2)}) collective-permute-start(bf16[256,1032]{0,1:T(8,128)(2,1)S(1)} %concatenate.11), channel_id=1, source_target_pairs={{0,128},{128,256},{256,384},{384,0},{1,129},{129,257},{257,385},{3... | collective-permute-start | bytes 1585160 | tf_op jit(solution)/shard_map/ppermute | solution.py:413
  104.0 10.0 %collective-permute-start.2 = (bf16[256,1032]{0,1:T(8,128)(2,1)S(1)}, bf16[256,1032]{0,1:T(8,128)(2,1)S(1)}, u32[]{:S(2)}, u32[]{:S(2)}) collective-permute-start(bf16[256,1032]{0,1:T(8,128)(2,1)S(1)} %collective-permute-done.1), channel_id=1, source_target_pairs={{0,1},{1,0},{2,3},{3,2},{4,5},{5,4},{6,7},{7,6},{8,9},{9,8},{10,11... | collective-permute-start | bytes 1585160 | tf_op jit(solution)/shard_map/ppermute | solution.py:407
Sparse Core Ops, SparseCore 0:
  34.1 71.0 all-gather.1

commit v6 on v5

--- a/solution.py
+++ b/solution.py
@@ -80,7 +80,7 @@
     for section in range(sizes[0]):
         for core in range(2):
             grid = index[section, :, :, core]
-            groups += (grid if (core == 0) == first else grid.T).tolist()
+            groups += (grid if (core == 1) == first else grid.T).tolist()
     return groups
 
 
@@ -292,15 +292,15 @@
     ring = CTX_SIDE
     block = half * 2 // (ring * ring)
 
+    @pl.when(core_ref[0] != 0)
+    def _():
+        rows_ref[0:half, :] = other_ref[0:half, :]
+        rows_ref[half : 2 * half, :] = own_ref[0:half, :]
+
     @pl.when(core_ref[0] == 0)
     def _():
-        rows_ref[0:half, :] = own_ref[0:half, :]
-        rows_ref[half : 2 * half, :] = other_ref[0:half, :]
-
-    @pl.when(core_ref[0] != 0)
-    def _():
         for outer in range(ring):
-            source = other_ref if outer < ring // 2 else own_ref
+            source = own_ref if outer < ring // 2 else other_ref
             for inner in range(ring):
                 start = ((outer % (ring // 2)) * ring + inner) * block
                 target = (inner * ring + outer) * block

time: 127 us -> 129 us (1.016)
  blocking collectives: 49.7 us -> 53.2 us
  starting transfers between devices: 21 us -> 18.7 us
    all_to_all x1, blocking collectives: 25.5 us -> 28.7 us  [weight_part(): lax.all_to_all(copies, ALL_AXES, 0, 0, axis_index_groups=crossed_groups(T...]
    ppermute x1, starting transfers between devices: 4.12 us -> 2.6 us  [from_behind(): lax.ppermute(value, axis, [(source, source + steps) for source in range(f...]
    ppermute x1, starting transfers between devices: 8.5 us -> 7.14 us  [other_half(): return lax.ppermute(x, axis, [(0, 1), (1, 0)])]
where the time goes in v6:
time: 129 us; the launch traced here: 128 us
  blocking collectives  53.2 us (41%)
  waiting for transfers between devices  21.2 us (16%)
  starting transfers between devices  18.7 us (14%)
  between operations  13.6 us (11%)
  Pallas kernels  11 us (9%)
  local copies, waits for them, and re-layouts  5.49 us (4%)
  other arithmetic  2.99 us (2%)
  matrix products  2.02 us (2%)
    all_to_all x1, blocking collectives, weight_part(): lax.all_to_all(copies, ALL_AXES, 0, 0, axis_index_groups=crossed_groups(T...  28.7 us
    all_to_all x1, blocking collectives, scanned_slices(): pieces = lax.all_to_all(sent, axes, 0, 0, tiled=True)  24.5 us
    all_to_all x1, waiting for transfers between devices, section_block(): lax.all_to_all(prior, CTX, 0, 0, tiled=True)  10.5 us
    ppermute x1, waiting for transfers between devices, shifted(): return lax.ppermute(value, axis, pairs)  9.16 us
    ppermute x1, starting transfers between devices, other_half(): return lax.ppermute(x, axis, [(0, 1), (1, 0)])  7.14 us
    all_to_all x1, starting transfers between devices, section_block(): lax.all_to_all(prior, CTX, 0, 0, tiled=True)  5.85 us
    pallas_call x1, Pallas kernels, projected(): pl.pallas_call(project_kernel, out_shape=jax.ShapeDtypeStruct((tokens, wi...  4.81 us
    unnamed x12, local copies, waits for them, and re-layouts  3.36 us
  transfers between devices with their start and end apart: 5, of which 3 were waited for; matrix products, arithmetic and copies ran while one was open for 6% of the time, Pallas kernels for 3%

profile of v6, /device:TPU:1, one launch (start us, length us, event | category | flops | bytes accessed | tf_op | source)
XLA Modules:
  0.0 128.2 jit_solution(15265308049582751203)
XLA Ops:
  6.5 1.9 %shard_map.114 = bf16[8,32,2048]{2,1,0:T(8,128)(2,1)} custom-call(bf16[32,2048]{1,0:T(8,128)(2,1)} %bitcast.75), custom_call_target="tpu_custom_call" | custom-call | bytes 1179648 | tf_op jit(solution)/shard_map/pallas_call | solution.py:139
  8.5 28.7 %all_to_all.15 = bf16[8,32,2048]{2,1,0:T(8,128)(2,1)} all-to-all(bf16[8,32,2048]{2,1,0:T(8,128)(2,1)} %shard_map.114), channel_id=1, replica_groups={{0,16,32,48,64,80,96,112},{2,18,34,50,66,82,98,114},{4,20,36,52,68,84,1..., dimensions={0} | all-to-all | bytes 2097152 | tf_op jit(solution)/shard_map/all_to_all | solution.py:156
  37.2 1.3 %shard_map.110 = bf16[8,1280]{1,0:T(8,128)(2,1)} custom-call(bf16[256,1024]{1,0:T(8,128)(2,1)} %bitcast.63, bf16[256,256]{1,0:T(8,128)(2,1)} %bitcast.67), custom_call_target="tpu_custom_call" | custom-call | bytes 40960 | tf_op jit(solution)/shard_map/pallas_call | solution.py:96
  38.6 2.6 %collective-permute-start = (bf16[8,1280]{1,0:T(8,128)(2,1)}, bf16[8,1280]{1,0:T(8,128)(2,1)S(1)}, u32[]{:S(2)}, u32[]{:S(2)}) collective-permute-start(bf16[8,1280]{1,0:T(8,128)(2,1)} %shard_map.110), channel_id=1, source_target_pairs={{0,2},{2,4},{4,6},{6,8},{8,10},{10,12},{12,14},{14,16},{16,18},{18... | collective-permute-start | bytes 61448 | tf_op jit(solution)/shard_map/ppermute | solution.py:34
  41.4 0.7 negate_bitcast_fusion
  42.0 0.8 compare_select_fusion
  42.8 0.2 fusion.14
  43.0 0.3 exponential_reduce_fusion
  43.5 0.8 exponential_bitcast_fusion
  44.4 1.0 copy-done
  45.4 0.9 copy-done.1
  46.4 0.7 copy-done.2
  47.1 0.7 copy-done.3
  47.8 0.3 shard_map.109
  48.1 1.1 shard_map.111
  49.3 24.5 %all_to_all.16.pieces_ref = bf16[64,2,1152]{2,1,0:T(2,128)(2,1)S(1)} all-to-all(bf16[64,2,1152]{2,1,0:T(2,128)(2,1)S(1)} %get-tuple-element.25), channel_id=1, replica_groups=mesh['section'=4,'ctx_0'=8,'ctx_1'=8,'mp'=2] {'ctx_0','ctx_1'}, dimensions={0} | all-to-all | bytes 589824 | tf_op jit(solution)/shard_map/all_to_all | solution.py:60
  73.8 1.1 shard_map.112
  74.8 5.9 %all-to-all-start.1 = ((bf16[64,16,128]{2,1,0:T(8,128)(2,1)}), bf16[64,16,128]{2,1,0:T(8,128)(2,1)S(1)}, u32[]{:S(2)}, u32[]{:S(2)}) async-start(bf16[64,16,128]{2,1,0:T(8,128)(2,1)} %shard_map.112), calls=%async_computation.1 | async-start | bytes 524288 | tf_op jit(solution)/shard_map/all_to_all | solution.py:469
  80.7 1.3 copy.17
  81.9 0.2 fusion.16
  82.1 0.3 convert_multiply_fusion
  82.5 1.4 %fusion.9 = f32[1,256,16,64]{1,3,2,0:T(8,128)S(1)} fusion(bf16[256,16,64]{0,2,1:T(8,128)(2,1)S(1)} %bitcast.71, f32[16,256]{1,0:T(8,128)S(1)} %compare_select_fusion, f32[16,256]{1,0:T(8,128)S(1)} %fusion.14, f32[256,256]{1,0:T(8,128)S(1)} %fusion.16, pred[256,256]{1,0:T(8,128)(4,1)S(1)} %iota_compare_fusion, bf16[1,256,16,64]{1,3,2,0:T(8,128)(2,1)S(1)} %bitcast.72, ...), kind=kOutput, calls=%fused_computation.11 | convolution fusion | flops 141295616 | bytes 2457664 | tf_op jit(solution)/shard_map/hcts,cshp->cthp/dot_general | solution.py:481
  83.9 10.5 %all-to-all-done.1 = bf16[64,16,128]{2,1,0:T(8,128)(2,1)S(1)} async-done(((bf16[64,16,128]{2,1,0:T(8,128)(2,1)}), bf16[64,16,128]{2,1,0:T(8,128)(2,1)S(1)}, u32[]{:S(2)}, u32[]{:S(2)}) %all-to-all-start.1) | async-done | bytes 262176 | tf_op jit(solution)/shard_map/all_to_all | solution.py:469
  94.4 0.3 fusion.10
  94.7 0.3 multiply_reduce_fusion
  95.0 0.2 concatenate.11
  95.1 3.1 %collective-permute-start.1 = (bf16[256,1032]{0,1:T(8,128)(2,1)S(1)}, bf16[256,1032]{0,1:T(8,128)(2,1)S(1)}, u32[]{:S(2)}, u32[]{:S(2)}) collective-permute-start(bf16[256,1032]{0,1:T(8,128)(2,1)S(1)} %concatenate.11), channel_id=1, source_target_pairs={{0,128},{128,256},{256,384},{384,0},{1,129},{129,257},{257,385},{3... | collective-permute-start | bytes 1585160 | tf_op jit(solution)/shard_map/ppermute | solution.py:413
  98.3 9.2 %collective-permute-done.1 = bf16[256,1032]{0,1:T(8,128)(2,1)S(1)} collective-permute-done((bf16[256,1032]{0,1:T(8,128)(2,1)S(1)}, bf16[256,1032]{0,1:T(8,128)(2,1)S(1)}, u32[]{:S(2)}, u32[]{:S(2)}) %collective-permute-start.1) | collective-permute-done | bytes 528416 | tf_op jit(solution)/shard_map/ppermute | solution.py:413
  107.4 7.1 %collective-permute-start.2 = (bf16[256,1032]{0,1:T(8,128)(2,1)S(1)}, bf16[256,1032]{0,1:T(8,128)(2,1)S(1)}, u32[]{:S(2)}, u32[]{:S(2)}) collective-permute-start(bf16[256,1032]{0,1:T(8,128)(2,1)S(1)} %collective-permute-done.1), channel_id=1, source_target_pairs={{0,1},{1,0},{2,3},{3,2},{4,5},{5,4},{6,7},{7,6},{8,9},{9,8},{10,11... | collective-permute-start | bytes 1585160 | tf_op jit(solution)/shard_map/ppermute | solution.py:407
  114.6 1.5 %collective-permute-done.2 = bf16[256,1032]{0,1:T(8,128)(2,1)S(1)} collective-permute-done((bf16[256,1032]{0,1:T(8,128)(2,1)S(1)}, bf16[256,1032]{0,1:T(8,128)(2,1)S(1)}, u32[]{:S(2)}, u32[]{:S(2)}) %collective-permute-start.2) | collective-permute-done | bytes 528416 | tf_op jit(solution)/shard_map/ppermute | solution.py:407
  116.1 0.4 shard_map.113
  116.6 4.8 %shard_map.115 = bf16[256,2048]{1,0:T(8,128)(2,1)} custom-call(bf16[256,2048]{1,0:T(8,128)(2,1)S(1)} %get-tuple-element.35.features_ref, f32[256,128]{1,0:T(8,128)S(1)} %get-tuple-element.36.scale_ref, bf16[2048,2048]{1,0:T(8,128)(2,1)} %all-gather.2.cloned.1.call-done.weight_ref), custom_call_target="tpu_custom_call" | custom-call | flops 2147483648 | bytes 8388608 | tf_op jit(solution)/shard_map/pallas_call | solution.py:387
  (26 shorter events, 0.6 us)
Async XLA Ops:
  6.5 110.0 %all-gather.2.cloned.1.call-start = ((), (), s32[]{:S(2)}) async-start(), calls=%async_computation.3 | async-start | bytes 9437184 | tf_op jit(solution)/shard_map/all_gather | solution.py:284
  38.6 43.9 %copy-start.5 = (f32[1,16]{1,0:T(1,128)S(1)}, f32[1,16]{1,0:T(1,128)}, u32[]{:S(2)}) copy-start(f32[1,16]{1,0:T(1,128)} %param.17) | copy-start | bytes 196
  38.6 9.5 %collective-permute-start = (bf16[8,1280]{1,0:T(8,128)(2,1)}, bf16[8,1280]{1,0:T(8,128)(2,1)S(1)}, u32[]{:S(2)}, u32[]{:S(2)}) collective-permute-start(bf16[8,1280]{1,0:T(8,128)(2,1)} %shard_map.110), channel_id=1, source_target_pairs={{0,2},{2,4},{4,6},{6,8},{8,10},{10,12},{12,14},{14,16},{16,18},{18... | collective-permute-start | bytes 61448 | tf_op jit(solution)/shard_map/ppermute | solution.py:34
  44.4 1.0 copy-start
  45.4 0.9 copy-start.1
  46.4 0.7 copy-start.2
  47.1 0.7 copy-start.3
  74.8 19.5 %all-to-all-start.1 = ((bf16[64,16,128]{2,1,0:T(8,128)(2,1)}), bf16[64,16,128]{2,1,0:T(8,128)(2,1)S(1)}, u32[]{:S(2)}, u32[]{:S(2)}) async-start(bf16[64,16,128]{2,1,0:T(8,128)(2,1)} %shard_map.112), calls=%async_computation.1 | async-start | bytes 524288 | tf_op jit(solution)/shard_map/all_to_all | solution.py:469
  82.5 12.2 %copy-start.4 = (f32[1,1024]{1,0:T(1,128)S(1)}, f32[1,1024]{1,0:T(1,128)}, u32[]{:S(2)}) copy-start(f32[1,1024]{1,0:T(1,128)} %param.20) | copy-start | bytes 12292
  95.1 12.3 %collective-permute-start.1 = (bf16[256,1032]{0,1:T(8,128)(2,1)S(1)}, bf16[256,1032]{0,1:T(8,128)(2,1)S(1)}, u32[]{:S(2)}, u32[]{:S(2)}) collective-permute-start(bf16[256,1032]{0,1:T(8,128)(2,1)S(1)} %concatenate.11), channel_id=1, source_target_pairs={{0,128},{128,256},{256,384},{384,0},{1,129},{129,257},{257,385},{3... | collective-permute-start | bytes 1585160 | tf_op jit(solution)/shard_map/ppermute | solution.py:413
  107.4 8.7 %collective-permute-start.2 = (bf16[256,1032]{0,1:T(8,128)(2,1)S(1)}, bf16[256,1032]{0,1:T(8,128)(2,1)S(1)}, u32[]{:S(2)}, u32[]{:S(2)}) collective-permute-start(bf16[256,1032]{0,1:T(8,128)(2,1)S(1)} %collective-permute-done.1), channel_id=1, source_target_pairs={{0,1},{1,0},{2,3},{3,2},{4,5},{5,4},{6,7},{7,6},{8,9},{9,8},{10,11... | collective-permute-start | bytes 1585160 | tf_op jit(solution)/shard_map/ppermute | solution.py:407
Sparse Core Ops, SparseCore 0:
  37.4 66.7 all-gather.1
